TPU v7x, 16 devices: a whole 2x2x2 slice. The times are simulated.
16 devices in a mesh: stage: 2 (over z), expert: 8 (over y, x, core).
Axes of the slice: x: 2, y: 2, z: 2, core: 2. Of those that a mesh axis runs over, the one named last changes fastest.
Arguments:
- x_act: bfloat16 [2, 16384, 1024], P('stage', 'expert')
- route_idx: int32 [2, 16384, 1], P('stage', 'expert')
- route_gate: float32 [2, 16384, 1], P('stage', 'expert')
- w_in1: bfloat16 [2, 128, 1024, 384], P('stage', 'expert')
- w_in3: bfloat16 [2, 128, 1024, 384], P('stage', 'expert')
- w_out: bfloat16 [2, 128, 384, 1024], P('stage', 'expert')
- ws_in1: bfloat16 [2, 1024, 384], P('stage')
- ws_in3: bfloat16 [2, 1024, 384], P('stage')
- ws_out: bfloat16 [2, 384, 1024], P('stage')
- dy_out: bfloat16 [2, 16384, 1024], P('stage', 'expert')
Outputs:
- output 1: bfloat16 [2, 16384, 1024], P('stage', 'expert')
- output 2: bfloat16 [2, 16384, 1024], P('stage', 'expert')
- output 3: bfloat16 [2, 128, 1024, 384], P('stage', 'expert')
- output 4: bfloat16 [2, 128, 1024, 384], P('stage', 'expert')
- output 5: bfloat16 [2, 128, 384, 1024], P('stage', 'expert')
- output 6: bfloat16 [2, 1024, 384], P('stage')
- output 7: bfloat16 [2, 1024, 384], P('stage')
- output 8: bfloat16 [2, 384, 1024], P('stage')
All inputs are finite; a program needn't handle non-finite values.
Results may differ from a plain program's by a relative error of at most 0.00662985.
Values are sent between devices in bfloat16 or wider.
A program may use at most 1 GiB of HBM per device.

v0:
```python
import jax
import jax.numpy as jnp
from jax import lax
from jax.sharding import PartitionSpec as P


def ragged_rows(lhs, rhs, group_sizes, rhs_contract):
    numbers = lax.RaggedDotDimensionNumbers(dot_dimension_numbers=(([1], [rhs_contract]), ([], [])), lhs_ragged_dimensions=[0], rhs_group_dimensions=[0])
    return lax.ragged_dot_general(lhs, rhs, group_sizes, numbers, preferred_element_type=jnp.float32)


def ragged_outer(lhs, rhs, group_sizes):
    numbers = lax.RaggedDotDimensionNumbers(dot_dimension_numbers=(([0], [0]), ([], [])), lhs_ragged_dimensions=[0], rhs_group_dimensions=[])
    return lax.ragged_dot_general(lhs, rhs, group_sizes, numbers, preferred_element_type=jnp.float32)


def expert_pass(x_rows, dy_rows, gate_rows, is_valid, group_sizes, w_one, w_three, w_two):
    pre_a = ragged_rows(x_rows, w_one, group_sizes, 1)
    pre_b = ragged_rows(x_rows, w_three, group_sizes, 1)
    sig_a = jax.nn.sigmoid(pre_a)
    act_a = pre_a * sig_a
    hidden = (act_a * pre_b).astype(jnp.bfloat16)
    out_rows = ragged_rows(hidden, w_two, group_sizes, 1)
    contrib = jnp.where(is_valid, gate_rows * out_rows, 0.0)
    grad_out = jnp.where(is_valid, gate_rows * dy_rows.astype(jnp.float32), 0.0).astype(jnp.bfloat16)
    grad_hid = ragged_rows(grad_out, w_two, group_sizes, 2)
    grad_a = jnp.where(is_valid, grad_hid * pre_b * sig_a * (1.0 + pre_a * (1.0 - sig_a)), 0.0).astype(jnp.bfloat16)
    grad_b = jnp.where(is_valid, grad_hid * act_a, 0.0).astype(jnp.bfloat16)
    dx_rows = jnp.where(is_valid, ragged_rows(grad_a, w_one, group_sizes, 2) + ragged_rows(grad_b, w_three, group_sizes, 2), 0.0)
    gw_one = ragged_outer(x_rows, grad_a, group_sizes)
    gw_three = ragged_outer(x_rows, grad_b, group_sizes)
    gw_two = ragged_outer(hidden, grad_out, group_sizes)
    return contrib, dx_rows, gw_one, gw_three, gw_two


def shared_pass(x_tok, dy_tok, w_one, w_three, w_two):
    pre_a = jnp.dot(x_tok, w_one, preferred_element_type=jnp.float32)
    pre_b = jnp.dot(x_tok, w_three, preferred_element_type=jnp.float32)
    sig_a = jax.nn.sigmoid(pre_a)
    act_a = pre_a * sig_a
    hidden = (act_a * pre_b).astype(jnp.bfloat16)
    out_tok = jnp.dot(hidden, w_two, preferred_element_type=jnp.float32)
    grad_hid = jnp.einsum('td,fd->tf', dy_tok, w_two, preferred_element_type=jnp.float32)
    grad_a = (grad_hid * pre_b * sig_a * (1.0 + pre_a * (1.0 - sig_a))).astype(jnp.bfloat16)
    grad_b = (grad_hid * act_a).astype(jnp.bfloat16)
    dx_tok = jnp.einsum('tf,df->td', grad_a, w_one, preferred_element_type=jnp.float32) + jnp.einsum('tf,df->td', grad_b, w_three, preferred_element_type=jnp.float32)
    gw_one = jnp.einsum('td,tf->df', x_tok, grad_a, preferred_element_type=jnp.float32)
    gw_three = jnp.einsum('td,tf->df', x_tok, grad_b, preferred_element_type=jnp.float32)
    gw_two = jnp.einsum('tf,td->fd', hidden, dy_tok, preferred_element_type=jnp.float32)
    return out_tok, dx_tok, gw_one, gw_three, gw_two


def solution(mesh):
    n_stage = mesh.shape['stage']
    n_group = mesh.shape['expert']
    fwd_perm = [(src, (src + 1) % n_stage) for src in range(n_stage)]
    back_perm = [((src + 1) % n_stage, src) for src in range(n_stage)]
    tok_spec = P('stage', 'expert', None)
    w_spec = P('stage', 'expert', None, None)
    sh_spec = P('stage', None, None)

    def device_fn(x_act, route_idx, route_gate, w_in1, w_in3, w_out, ws_in1, ws_in3, ws_out, dy_out):
        x_tok = lax.ppermute(x_act[0], 'stage', fwd_perm)
        idx_tok = lax.ppermute(route_idx[0], 'stage', fwd_perm)
        gate_tok = lax.ppermute(route_gate[0], 'stage', fwd_perm)
        dy_tok = dy_out[0]
        n_tok = x_tok.shape[0]
        top_k = idx_tok.shape[1]
        n_local = w_in1.shape[1]
        row_cap = min(top_k, n_group) * n_tok // n_group
        n_slot = n_group * row_cap
        dest_dev = idx_tok // n_local
        dev_ids = jnp.arange(n_group, dtype=jnp.int32)
        dev_hits = jnp.any(dest_dev[:, :, None] == dev_ids, axis=1)
        slot_rank = jnp.cumsum(dev_hits.astype(jnp.int32), axis=0) - 1
        flat_slot = jnp.where(dev_hits, dev_ids * row_cap + slot_rank, n_slot)
        tok_ids = jnp.broadcast_to(jnp.arange(n_tok, dtype=jnp.int32)[:, None], (n_tok, n_group))
        slot_tok = jnp.full((n_slot + 1,), n_tok, jnp.int32).at[flat_slot.reshape(-1)].set(tok_ids.reshape(-1))[:n_slot]
        safe_tok = jnp.minimum(slot_tok, n_tok - 1)
        slot_dev = jnp.arange(n_slot, dtype=jnp.int32) // row_cap
        on_dest = (dest_dev[safe_tok] == slot_dev[:, None]) & (slot_tok < n_tok)[:, None]
        send_lid = jnp.where(on_dest, idx_tok[safe_tok] % n_local, -1)
        send_gate = jnp.where(on_dest, gate_tok[safe_tok], 0.0)
        recv_x = lax.all_to_all(x_tok[safe_tok], 'expert', 0, 0, tiled=True)
        recv_lid = lax.all_to_all(send_lid, 'expert', 0, 0, tiled=True)
        recv_gate = lax.all_to_all(send_gate, 'expert', 0, 0, tiled=True)
        recv_dy = lax.all_to_all(dy_tok[safe_tok], 'expert', 0, 0, tiled=True)
        pair_key = jnp.where(recv_lid >= 0, recv_lid, n_local).reshape(-1)
        pair_order = jnp.argsort(pair_key, stable=True)
        group_sizes = jnp.zeros((n_local + 1,), jnp.int32).at[pair_key].add(1)[:n_local]
        row_of_pair = pair_order // top_k
        is_valid = (pair_key[pair_order] < n_local)[:, None]
        gate_rows = recv_gate.reshape(-1)[pair_order][:, None]
        contrib, dx_rows, gw_one, gw_three, gw_two = expert_pass(
            recv_x[row_of_pair], recv_dy[row_of_pair], gate_rows, is_valid, group_sizes, w_in1[0], w_in3[0], w_out[0])
        part_y = jax.ops.segment_sum(contrib, row_of_pair, num_segments=n_slot).astype(jnp.bfloat16)
        part_dx = jax.ops.segment_sum(dx_rows, row_of_pair, num_segments=n_slot).astype(jnp.bfloat16)
        back_y = lax.all_to_all(part_y, 'expert', 0, 0, tiled=True)
        back_dx = lax.all_to_all(part_dx, 'expert', 0, 0, tiled=True)
        y_moe = jax.ops.segment_sum(back_y.astype(jnp.float32), slot_tok, num_segments=n_tok + 1)[:n_tok]
        dx_moe = jax.ops.segment_sum(back_dx.astype(jnp.float32), slot_tok, num_segments=n_tok + 1)[:n_tok]
        sh_out, sh_dx, gs_one, gs_three, gs_two = shared_pass(x_tok, dy_tok, ws_in1[0], ws_in3[0], ws_out[0])
        y_tok = (y_moe + sh_out).astype(jnp.bfloat16)
        dx_tok = lax.ppermute((dx_moe + sh_dx).astype(jnp.bfloat16), 'stage', back_perm)
        gs_one = lax.psum(gs_one, 'expert')
        gs_three = lax.psum(gs_three, 'expert')
        gs_two = lax.psum(gs_two, 'expert')
        return (y_tok[None], dx_tok[None], gw_one.astype(jnp.bfloat16)[None], gw_three.astype(jnp.bfloat16)[None],
                gw_two.astype(jnp.bfloat16)[None], gs_one.astype(jnp.bfloat16)[None], gs_three.astype(jnp.bfloat16)[None],
                gs_two.astype(jnp.bfloat16)[None])

    return jax.shard_map(device_fn, mesh=mesh,
                         in_specs=(tok_spec, tok_spec, tok_spec, w_spec, w_spec, w_spec, sh_spec, sh_spec, sh_spec, tok_spec),
                         out_specs=(tok_spec, tok_spec, w_spec, w_spec, w_spec, sh_spec, sh_spec, sh_spec),
                         check_vma=False)
```

profile of v0, /device:TPU:0, one launch (start us, length us, event | category | flops | bytes accessed | tf_op | source)
XLA Modules:
  0.0 910.8 jit_solution(2283174875149685124)
XLA Ops:
  0.6 3.3 collective-permute-start
  4.0 2.0 collective-permute-start.2
  6.7 2.3 reduce-window.6
  10.5 60.3 %scatter_custom_fusion = s32[2049]{0:T(1024)S(1)} fusion(s32[16384]{0:T(1024)S(1)} %bitcast.125, s32[16384]{0:T(1024)S(1)} %reshape.349, s32[]{:T(128)} %constant.75.clone.1), kind=kCustom, calls=%fused_computation.95 | custom fusion | bytes 8200 | tf_op jit(solution)/shard_map/scatter | solution.py:78
  71.5 11.8 %gather_fusion = s32[2048]{0:T(1024)S(1)} fusion(s32[2048]{0:T(1024)S(1)} %bitcast.104, s32[2048]{0:T(1024)S(1)} %get-tuple-element.97), kind=kCustom, calls=%fused_computation | custom fusion | bytes 24576 | tf_op jit(solution)/shard_map/gather | solution.py:81
  83.3 11.8 %gather_fusion.3 = f32[2048]{0:T(1024)S(1)} fusion(f32[2048]{0:T(1024)S(1)} %bitcast.107, s32[2048]{0:T(1024)S(1)} %get-tuple-element.97), kind=kCustom, calls=%fused_computation.3 | custom fusion | bytes 24576 | tf_op jit(solution)/shard_map/gather | solution.py:83
  95.1 11.8 %gather_fusion.1 = s32[2048]{0:T(1024)S(1)} fusion(s32[2048]{0:T(1024)S(1)} %bitcast.106, s32[2048]{0:T(1024)S(1)} %get-tuple-element.97), kind=kCustom, calls=%fused_computation.1 | custom fusion | bytes 24576 | tf_op jit(solution)/shard_map/gather | solution.py:82
  107.0 0.6 copy.56
  107.6 3.7 all-to-all-start
  111.3 0.6 copy.57
  111.9 3.9 all-to-all-done
  115.8 3.3 all-to-all-start.1
  119.1 13.7 %gather_fusion.7 = bf16[2048,1024]{1,0:T(8,128)(2,1)} fusion(bf16[2048,1024]{1,0:T(8,128)(2,1)} %bitcast.108, s32[2048]{0:T(1024)S(1)} %get-tuple-element.97), kind=kCustom, calls=%fused_computation.7 | custom fusion | bytes 8396800 | tf_op jit(solution)/shard_map/gather | solution.py:87
  132.8 4.6 all-to-all-start.4
  137.4 13.7 %gather_fusion.5 = bf16[2048,1024]{1,0:T(8,128)(2,1)} fusion(bf16[2048,1024]{1,0:T(8,128)(2,1)} %collective-permute-done.2, s32[2048]{0:T(1024)S(1)} %get-tuple-element.97), kind=kCustom, calls=%fused_computation.5 | custom fusion | bytes 8396800 | tf_op jit(solution)/shard_map/gather | solution.py:84
  151.0 35.3 %all-to-all-done.4 = bf16[8,256,1024]{2,1,0:T(8,128)(2,1)} async-done(((bf16[8,256,1024]{2,1,0:T(8,128)(2,1)}), bf16[8,256,1024]{2,1,0:T(8,128)(2,1)}, u32[]{:S(2)}, u32[]{:S(2)}) %all-to-all-start.4) | async-done | bytes 4194336 | tf_op jit(solution)/shard_map/all_to_all | solution.py:87
  186.4 4.5 all-to-all-start.2
  190.9 16.6 %copy.62 = bf16[1,16,384,1024]{2,3,1,0:T(8,128)(2,1)} copy(bf16[1,16,384,1024]{3,2,1,0:T(8,128)(2,1)} %param.15) | data formatting | bytes 25165824 | tf_op args[5]
  207.5 16.6 %copy.60 = bf16[1,16,1024,384]{2,3,1,0:T(8,128)(2,1)} copy(bf16[1,16,1024,384]{3,2,1,0:T(8,128)(2,1)} %param.14) | data formatting | bytes 25165824 | tf_op args[4]
  224.1 16.7 %copy.58 = bf16[1,16,1024,384]{2,3,1,0:T(8,128)(2,1)} copy(bf16[1,16,1024,384]{3,2,1,0:T(8,128)(2,1)} %param.13) | data formatting | bytes 25165824 | tf_op args[3]
  240.8 6.2 fusion.17
  247.0 15.2 %scatter_custom_fusion.1 = s32[17]{0:T(128)} fusion(s32[2048]{0:T(1024)S(1)} %bitcast.127, s32[2048]{0:T(1024)S(1)} %broadcast.247, s32[]{:T(128)} %constant.77.clone.1), kind=kCustom, calls=%fused_computation.101 | custom fusion | flops 2048 | bytes 72 | tf_op jit(solution)/shard_map/scatter-add | solution.py:90
  262.2 1.8 ragged-dot-metadata.1
  264.0 2.2 ragged-dot-metadata
  266.3 5.0 sort.17
  271.3 11.8 %gather_fusion.2 = s32[2048]{0:T(1024)S(1)} fusion(s32[2048]{0:T(1024)S(1)} %compare_select_fusion.4, s32[2048]{0:T(1024)S(1)} %fusion.34), kind=kCustom, calls=%fused_computation.2 | custom fusion | bytes 24576 | tf_op jit(solution)/shard_map/gather | solution.py:92
  283.1 11.8 %gather_fusion.4 = f32[2048]{0:T(1024)S(1)} fusion(f32[2048]{0:T(1024)S(1)} %bitcast.105, s32[2048]{0:T(1024)S(1)} %fusion.34), kind=kCustom, calls=%fused_computation.4 | custom fusion | bytes 24576 | tf_op jit(solution)/shard_map/gather | solution.py:93
  294.9 13.7 %gather_fusion.8 = bf16[2048,1024]{1,0:T(8,128)(2,1)} fusion(bf16[2048,1024]{1,0:T(8,128)(2,1)} %bitcast.29, s32[2048]{0:T(1024)S(1)} %fusion.34), kind=kCustom, calls=%fused_computation.8 | custom fusion | bytes 8396800 | tf_op jit(solution)/shard_map/gather | solution.py:95
  308.6 4.2 select_convert_fusion
  312.7 23.1 %ragged-dot-none.5 = f32[2048,384]{1,0:T(8,128)} custom-call(s32[1]{0:T(128)} %get-tuple-element.34, s32[17]{0:T(128)} %get-tuple-element.35, s32[23]{0:T(128)} %get-tuple-element.36, s32[23]{0:T(128)} %get-tuple-element.37, s32[1]{0:T(128)} %get-tuple-element.34, bf16[2048,1024]{1,0:T(8,128)(2,1)} %select_convert_fusion, bf16[16,1024,384]{2,1,0:T(8,128)(2,1)} %bitcast.116), custom_call_target="tpu_custom_call" | custom-call | flops 1610612736 | bytes 19923008 | tf_op ragged-dot-none
  335.9 6.2 fusion.21
  342.1 13.7 %gather_fusion.6 = bf16[2048,1024]{1,0:T(8,128)(2,1)} fusion(bf16[2048,1024]{1,0:T(8,128)(2,1)} %bitcast.14, s32[2048]{0:T(1024)S(1)} %fusion.34), kind=kCustom, calls=%fused_computation.6 | custom fusion | bytes 8396800 | tf_op jit(solution)/shard_map/gather | solution.py:95
  355.7 23.1 %ragged-dot-none.7 = f32[2048,384]{1,0:T(8,128)} custom-call(s32[1]{0:T(128)} %get-tuple-element.34, s32[17]{0:T(128)} %get-tuple-element.35, s32[23]{0:T(128)} %get-tuple-element.36, s32[23]{0:T(128)} %get-tuple-element.37, s32[1]{0:T(128)} %get-tuple-element.34, bf16[2048,1024]{1,0:T(8,128)(2,1)} %gather_fusion.6, bf16[16,1024,384]{2,1,0:T(8,128)(2,1)} %bitcast.111), custom_call_target="tpu_custom_call" | custom-call | flops 1610612736 | bytes 19923008 | tf_op jit(solution)/shard_map/ragged_dot_general/ragged-dot-none
  378.8 23.0 %ragged-dot-none.8 = f32[2048,384]{1,0:T(8,128)} custom-call(s32[1]{0:T(128)} %get-tuple-element.34, s32[17]{0:T(128)} %get-tuple-element.35, s32[23]{0:T(128)} %get-tuple-element.36, s32[23]{0:T(128)} %get-tuple-element.37, s32[1]{0:T(128)} %get-tuple-element.34, bf16[2048,1024]{1,0:T(8,128)(2,1)} %gather_fusion.6, bf16[16,1024,384]{2,1,0:T(8,128)(2,1)} %bitcast.112), custom_call_target="tpu_custom_call" | custom-call | flops 1610612736 | bytes 19923008 | tf_op jit(solution)/shard_map/ragged_dot_general/ragged-dot-none
  401.8 6.1 select_convert_fusion.1
  407.9 24.3 %ragged-dot-none.3 = f32[2048,1024]{1,0:T(8,128)} custom-call(s32[1]{0:T(128)} %get-tuple-element.34, s32[17]{0:T(128)} %get-tuple-element.35, s32[23]{0:T(128)} %get-tuple-element.36, s32[23]{0:T(128)} %get-tuple-element.37, s32[1]{0:T(128)} %get-tuple-element.34, bf16[2048,384]{1,0:T(8,128)(2,1)} %get-tuple-element.91, bf16[16,384,1024]{2,1,0:T(8,128)(2,1)} %bitcast.115), custom_call_target="tpu_custom_call" | custom-call | flops 1610612736 | bytes 22544448 | tf_op ragged-dot-none
  432.3 24.3 %ragged-dot-none.4 = f32[2048,1024]{1,0:T(8,128)} custom-call(s32[1]{0:T(128)} %get-tuple-element.34, s32[17]{0:T(128)} %get-tuple-element.35, s32[23]{0:T(128)} %get-tuple-element.36, s32[23]{0:T(128)} %get-tuple-element.37, s32[1]{0:T(128)} %get-tuple-element.34, bf16[2048,384]{1,0:T(8,128)(2,1)} %get-tuple-element.92, bf16[16,384,1024]{2,1,0:T(8,128)(2,1)} %bitcast.114), custom_call_target="tpu_custom_call" | custom-call | flops 1610612736 | bytes 22544448 | tf_op ragged-dot-none
  456.6 23.9 %scatter_custom_fusion.4 = f32[2048,1024]{1,0:T(8,128)} fusion(s32[2048]{0:T(1024)S(1)} %get-tuple-element.9, f32[]{:T(128)} %constant.74.clone.1, f32[2048,1024]{1,0:T(8,128)} %ragged-dot-none.4, f32[2048,1024]{1,0:T(8,128)} %ragged-dot-none.3, pred[2048]{0:T(1024)(128)(4,1)S(1)} %broadcast_compare_fusion), kind=kCustom, calls=%fused_computation.33 | custom fusion | flops 6291456 | bytes 25168896 | tf_op jit(solution)/shard_map/scatter-add | solution.py:97
  480.5 6.0 convert_element_type.82
  486.5 4.8 all-to-all-start.5
  491.3 7.8 multiply_convert_fusion
  499.1 6.3 convolution_bitcast_fusion
  505.4 5.3 convolution_bitcast_fusion.1
  510.7 3.0 fusion.41
  513.7 117.4 %all-reduce.2 = (bf16[1024,384]{0,1:T(8,128)(2,1)}, bf16[1024,384]{0,1:T(8,128)(2,1)}, bf16[384,1024]{1,0:T(8,128)(2,1)}) all-reduce(f32[1024,384]{0,1:T(8,128)} %convolution_bitcast_fusion.1, f32[1024,384]{0,1:T(8,128)} %convolution_bitcast_fusion, f32[384,1024]{1,0:T(8,128)} %fusion.41), channel_id=1, replica_groups=mesh['stage'=2,'expert'=8] {'expert'}, use_global_device_ids=true, to_apply=%region_9.10 | all-reduce | flops 1179648 | bytes 7077888 | tf_op jit(solution)/shard_map/psum | solution.py:105
  631.1 2.3 copy.64
  633.4 2.3 copy.65
  635.7 5.8 fusion.23
  641.4 24.5 %ragged-dot-none.6 = f32[2048,1024]{1,0:T(8,128)} custom-call(s32[1]{0:T(128)} %get-tuple-element.34, s32[17]{0:T(128)} %get-tuple-element.35, s32[23]{0:T(128)} %get-tuple-element.36, s32[23]{0:T(128)} %get-tuple-element.37, s32[1]{0:T(128)} %get-tuple-element.34, bf16[2048,384]{1,0:T(8,128)(2,1)} %get-tuple-element.93, bf16[16,384,1024]{2,1,0:T(8,128)(2,1)} %bitcast.113), custom_call_target="tpu_custom_call" | custom-call | flops 1610612736 | bytes 22544448 | tf_op jit(solution)/shard_map/ragged_dot_general/ragged-dot-none
  665.9 23.3 %scatter_custom_fusion.2 = f32[2048,1024]{1,0:T(8,128)} fusion(s32[2048]{0:T(1024)S(1)} %get-tuple-element.9, f32[2048,1024]{1,0:T(8,128)} %ragged-dot-none.6, f32[2048]{0:T(1024)S(1)} %gather_fusion.4, f32[]{:T(128)} %constant.74.clone.1, pred[2048]{0:T(1024)(128)(4,1)S(1)} %broadcast_compare_fusion), kind=kCustom, calls=%fused_computation.31 | custom fusion | flops 6291456 | bytes 16788480 | tf_op jit(solution)/shard_map/scatter-add | solution.py:96
  689.3 6.0 convert_element_type.73
  695.3 26.1 %ragged-dot-none.1 = f32[16,1024,384]{2,1,0:T(8,128)} custom-call(s32[1]{0:T(128)} %get-tuple-element.18, s32[17]{0:T(128)} %get-tuple-element.19, s32[23]{0:T(128)} %get-tuple-element.20, s32[23]{0:T(128)} %get-tuple-element.21, s32[1]{0:T(128)} %get-tuple-element.18, bf16[2048,1024]{1,0:T(8,128)(2,1)} %gather_fusion.6, bf16[2048,384]{1,0:T(8,128)(2,1)} %get-tuple-element.91), custom_call_target="tpu_custom_call" | custom-call | flops 1610612736 | bytes 30933056 | tf_op jit(solution)/shard_map/ragged_dot_general/ragged-dot-none
  721.4 26.2 %ragged-dot-none.2 = f32[16,1024,384]{2,1,0:T(8,128)} custom-call(s32[1]{0:T(128)} %get-tuple-element.18, s32[17]{0:T(128)} %get-tuple-element.19, s32[23]{0:T(128)} %get-tuple-element.20, s32[23]{0:T(128)} %get-tuple-element.21, s32[1]{0:T(128)} %get-tuple-element.18, bf16[2048,1024]{1,0:T(8,128)(2,1)} %gather_fusion.6, bf16[2048,384]{1,0:T(8,128)(2,1)} %get-tuple-element.92), custom_call_target="tpu_custom_call" | custom-call | flops 1610612736 | bytes 30933056 | tf_op jit(solution)/shard_map/ragged_dot_general/ragged-dot-none
  747.6 25.7 %ragged-dot-none = f32[16,384,1024]{2,1,0:T(8,128)} custom-call(s32[1]{0:T(128)} %get-tuple-element.18, s32[17]{0:T(128)} %get-tuple-element.19, s32[23]{0:T(128)} %get-tuple-element.20, s32[23]{0:T(128)} %get-tuple-element.21, s32[1]{0:T(128)} %get-tuple-element.18, bf16[2048,384]{1,0:T(8,128)(2,1)} %get-tuple-element.93, bf16[2048,1024]{1,0:T(8,128)(2,1)} %select_convert_fusion), custom_call_target="tpu_custom_call" | custom-call | flops 1610612736 | bytes 30933056 | tf_op jit(solution)/shard_map/ragged_dot_general/ragged-dot-none
  773.3 4.6 all-to-all-start.3
  777.9 22.2 %scatter_custom_fusion.5 = f32[2049,1024]{1,0:T(8,128)} fusion(s32[2048]{0:T(1024)} %get-tuple-element.98, bf16[2048,1024]{1,0:T(8,128)(2,1)} %bitcast.48, f32[]{:T(128)} %constant.74.clone.1), kind=kCustom, calls=%fused_computation.22 | custom fusion | flops 4194304 | bytes 12587520 | tf_op jit(solution)/shard_map/scatter-add | solution.py:101
  800.1 10.8 %fusion = bf16[2048,1024]{1,0:T(8,128)(2,1)} fusion(f32[2049,1024]{1,0:T(8,128)} %scatter_custom_fusion.5, f32[2048,1024]{1,0:T(8,128)} %fusion.23, bf16[2048,384]{1,0:T(8,128)(2,1)} %copy-done.4, bf16[1,1024,384]{2,1,0:T(8,128)(2,1)S(1)} %copy-done.5), kind=kOutput, calls=%fused_computation.19 | convolution fusion | flops 1616904192 | bytes 23330816 | tf_op jit(solution)/shard_map/tf,df->td/dot_general | solution.py:46
  810.9 3.5 collective-permute-start.3
  814.5 13.4 %convert_bitcast_fusion = bf16[1,16,384,1024]{3,2,1,0:T(8,128)(2,1)} fusion(f32[16,384,1024]{2,1,0:T(8,128)} %ragged-dot-none), kind=kLoop, calls=%fused_computation.15 | loop fusion | flops 6291456 | bytes 37748736 | tf_op jit(solution)/shard_map/broadcast_in_dim | solution.py:109
  827.9 18.5 %convert_bitcast_fusion.1 = (bf16[1,16,1024,384]{3,2,1,0:T(8,128)(2,1)}, bf16[1,16,1024,384]{3,2,1,0:T(8,128)(2,1)}) fusion(f32[16,1024,384]{2,1,0:T(8,128)S(1)} %bitcast.110, f32[16,1024,384]{2,1,0:T(8,128)} %ragged-dot-none.2), kind=kLoop, calls=%fused_computation.16 | loop fusion | flops 12582912 | bytes 75497472 | tf_op jit(solution)/shard_map/broadcast_in_dim | solution.py:108
  846.4 22.0 %scatter_custom_fusion.3 = f32[2049,1024]{1,0:T(8,128)} fusion(s32[2048]{0:T(1024)} %get-tuple-element.98, bf16[2048,1024]{1,0:T(8,128)(2,1)} %bitcast.44, f32[]{:T(128)} %constant.74.clone.1), kind=kCustom, calls=%fused_computation.24 | custom fusion | flops 4194304 | bytes 12587520 | tf_op jit(solution)/shard_map/scatter-add | solution.py:100
  868.4 7.7 fusion.14
  876.1 29.6 %collective-permute-done.3 = bf16[2048,1024]{1,0:T(8,128)(2,1)} collective-permute-done((bf16[2048,1024]{1,0:T(8,128)(2,1)}, bf16[2048,1024]{1,0:T(8,128)(2,1)}, u32[]{:S(2)}, u32[]{:S(2)}) %collective-permute-start.3) | collective-permute-done | bytes 4194336 | tf_op jit(solution)/shard_map/ppermute | solution.py:104
  905.7 4.6 copy.78
  (63 shorter events, 3.0 us)
Async XLA Ops:
  0.6 490.6 %copy-start = (bf16[1,1024,384]{2,1,0:T(8,128)(2,1)S(1)}, bf16[1,1024,384]{2,1,0:T(8,128)(2,1)}, u32[]{:S(2)}) copy-start(bf16[1,1024,384]{2,1,0:T(8,128)(2,1)} %param.16) | copy-start | bytes 2359300
  0.6 6.0 collective-permute-start
  4.0 79.3 %collective-permute-start.1 = (f32[2048,1]{0,1:T(1,128)}, f32[2048,1]{0,1:T(1,128)S(1)}, u32[]{:S(2)}, u32[]{:S(2)}) collective-permute-start(f32[2048,1]{0,1:T(1,128)} %bitcast.131), channel_id=1, source_target_pairs={{0,8},{8,0},{1,9},{9,1},{2,10},{10,2},{3,11},{11,3},{4,12},{12,4},... | collective-permute-start | bytes 24584 | tf_op jit(solution)/shard_map/ppermute | solution.py:65
  4.0 133.3 %collective-permute-start.2 = (bf16[2048,1024]{1,0:T(8,128)(2,1)}, bf16[2048,1024]{1,0:T(8,128)(2,1)}, u32[]{:S(2)}, u32[]{:S(2)}) collective-permute-start(bf16[2048,1024]{1,0:T(8,128)(2,1)} %bitcast.128), channel_id=1, source_target_pairs={{0,8},{8,0},{1,9},{9,1},{2,10},{10,2},{3,11},{11,3},{4,12},{12,4},... | collective-permute-start | bytes 12582920 | tf_op jit(solution)/shard_map/ppermute | solution.py:63
  107.6 8.2 all-to-all-start
  115.8 17.0 %all-to-all-start.1 = ((f32[8,256,1]{1,2,0:T(1,128)}), f32[8,256,1]{1,2,0:T(1,128)S(1)}, u32[]{:S(2)}, u32[]{:S(2)}) async-start(f32[8,256,1]{1,2,0:T(1,128)} %copy.57), calls=%async_computation.1 | async-start | bytes 16384 | tf_op jit(solution)/shard_map/all_to_all | solution.py:86
  132.8 53.6 %all-to-all-start.4 = ((bf16[8,256,1024]{2,1,0:T(8,128)(2,1)}), bf16[8,256,1024]{2,1,0:T(8,128)(2,1)}, u32[]{:S(2)}, u32[]{:S(2)}) async-start(bf16[8,256,1024]{2,1,0:T(8,128)(2,1)} %bitcast.120), calls=%async_computation.4 | async-start | bytes 8388608 | tf_op jit(solution)/shard_map/all_to_all | solution.py:87
  186.4 155.7 %all-to-all-start.2 = ((bf16[8,256,1024]{2,1,0:T(8,128)(2,1)}), bf16[8,256,1024]{2,1,0:T(8,128)(2,1)}, u32[]{:S(2)}, u32[]{:S(2)}) async-start(bf16[8,256,1024]{2,1,0:T(8,128)(2,1)} %bitcast.117), calls=%async_computation.2 | async-start | bytes 8388608 | tf_op jit(solution)/shard_map/all_to_all | solution.py:84
  224.1 16.7 %copy-start.6 = (bf16[1,384,1024]{2,1,0:T(8,128)(2,1)S(1)}, bf16[1,384,1024]{2,1,0:T(8,128)(2,1)}, u32[]{:S(2)}) copy-start(bf16[1,384,1024]{2,1,0:T(8,128)(2,1)} %param.18) | copy-start | bytes 2359300
  312.7 23.1 %copy-start.5 = (bf16[1,1024,384]{2,1,0:T(8,128)(2,1)S(1)}, bf16[1,1024,384]{2,1,0:T(8,128)(2,1)}, u32[]{:S(2)}) copy-start(bf16[1,1024,384]{2,1,0:T(8,128)(2,1)} %param.17) | copy-start | bytes 2359300
  486.5 286.8 %all-to-all-start.5 = ((bf16[8,256,1024]{2,1,0:T(8,128)(2,1)}), bf16[8,256,1024]{2,1,0:T(8,128)(2,1)}, u32[]{:S(2)}, u32[]{:S(2)}) async-start(bf16[8,256,1024]{2,1,0:T(8,128)(2,1)} %bitcast.118), calls=%async_computation.5 | async-start | bytes 8388608 | tf_op jit(solution)/shard_map/all_to_all | solution.py:99
  499.1 6.3 copy-start.4
  499.1 11.6 %copy-start.2 = (bf16[2048,384]{1,0:T(8,128)(2,1)}, bf16[2048,384]{1,0:T(8,128)(2,1)S(1)}, u32[]{:S(2)}) copy-start(bf16[2048,384]{1,0:T(8,128)(2,1)S(1)} %get-tuple-element.96) | copy-start | bytes 4718596
  505.4 5.3 copy-start.1
  773.3 73.1 %all-to-all-start.3 = ((bf16[8,256,1024]{2,1,0:T(8,128)(2,1)}), bf16[8,256,1024]{2,1,0:T(8,128)(2,1)}, u32[]{:S(2)}, u32[]{:S(2)}) async-start(bf16[8,256,1024]{2,1,0:T(8,128)(2,1)} %bitcast.119), calls=%async_computation.3 | async-start | bytes 8388608 | tf_op jit(solution)/shard_map/all_to_all | solution.py:98
  800.1 27.8 %slice-start = ((s8[25165824]{0:T(1024)(128)(4,1)}), s8[4194304]{0:T(1024)(128)(4,1)S(1)}, s32[]{:S(2)}) async-start(s8[25165824]{0:T(1024)(128)(4,1)} %bitcast.109), calls=%async_computation.6 | async-start | bytes 8388608
  800.1 27.8 %slice-start.1 = ((s8[25165824]{0:T(1024)(128)(4,1)}), s8[4194304]{0:T(1024)(128)(4,1)S(1)}, s32[]{:S(2)}) async-start(s8[25165824]{0:T(1024)(128)(4,1)} %bitcast.109), calls=%async_computation.7 | async-start | bytes 8388608
  800.1 27.8 %slice-start.2 = ((s8[25165824]{0:T(1024)(128)(4,1)}), s8[4194304]{0:T(1024)(128)(4,1)S(1)}, s32[]{:S(2)}) async-start(s8[25165824]{0:T(1024)(128)(4,1)} %bitcast.109), calls=%async_computation.8 | async-start | bytes 8388608
  810.9 17.0 %slice-start.3 = ((s8[25165824]{0:T(1024)(128)(4,1)}), s8[4194304]{0:T(1024)(128)(4,1)S(1)}, s32[]{:S(2)}) async-start(s8[25165824]{0:T(1024)(128)(4,1)} %bitcast.109), calls=%async_computation.9 | async-start | bytes 8388608
  810.9 17.0 %slice-start.4 = ((s8[25165824]{0:T(1024)(128)(4,1)}), s8[4194304]{0:T(1024)(128)(4,1)S(1)}, s32[]{:S(2)}) async-start(s8[25165824]{0:T(1024)(128)(4,1)} %bitcast.109), calls=%async_computation.10 | async-start | bytes 8388608
  810.9 17.0 %slice-start.5 = ((s8[25165824]{0:T(1024)(128)(4,1)}), s8[4194304]{0:T(1024)(128)(4,1)S(1)}, s32[]{:S(2)}) async-start(s8[25165824]{0:T(1024)(128)(4,1)} %bitcast.109), calls=%async_computation.11 | async-start | bytes 8388608
  810.9 94.8 %collective-permute-start.3 = (bf16[2048,1024]{1,0:T(8,128)(2,1)}, bf16[2048,1024]{1,0:T(8,128)(2,1)}, u32[]{:S(2)}, u32[]{:S(2)}) collective-permute-start(bf16[2048,1024]{1,0:T(8,128)(2,1)} %fusion), channel_id=1, source_target_pairs={{8,0},{0,8},{9,1},{1,9},{10,2},{2,10},{11,3},{3,11},{12,4},{4,12},... | collective-permute-start | bytes 12582920 | tf_op jit(solution)/shard_map/ppermute | solution.py:104
  846.4 22.0 %copy-start.3 = (bf16[2048,384]{1,0:T(8,128)(2,1)S(1)}, bf16[2048,384]{1,0:T(8,128)(2,1)}, u32[]{:S(2)}) copy-start(bf16[2048,384]{1,0:T(8,128)(2,1)} %copy-done.2) | copy-start | bytes 4718596
  846.4 22.0 %copy-start.7 = (bf16[1,384,1024]{2,1,0:T(8,128)(2,1)S(1)}, bf16[1,384,1024]{2,1,0:T(8,128)(2,1)}, u32[]{:S(2)}) copy-start(bf16[1,384,1024]{2,1,0:T(8,128)(2,1)} %param.18) | copy-start | bytes 2359300
where the time goes:
time: 926 us; the launch traced here: 911 us
  local copies, waits for them, and re-layouts  236 us (25%)
  Pallas kernels  224 us (24%)
  other arithmetic  169 us (18%)
  blocking collectives  117 us (13%)
  waiting for transfers between devices  68.8 us (7%)
  matrix products  59 us (6%)
  starting transfers between devices  34.4 us (4%)
    another operation x6, Pallas kernels  149 us
    psum x1, blocking collectives, device_fn(): gs_one = lax.psum(gs_one, 'expert')  117 us
    unnamed x5, Pallas kernels  75.8 us
    scatter x1, local copies, waits for them, and re-layouts, device_fn(): jnp.full((n_slot + 1,), n_tok, jnp.int32).at[flat_slot.reshape(-1)]  60.3 us
    unnamed x34, local copies, waits for them, and re-layouts  59.1 us
    all_to_all x1, waiting for transfers between devices, device_fn(): recv_dy = lax.all_to_all(dy_tok[safe_tok], 'expert', 0, 0, tiled=True)  35.3 us
    ppermute x1, waiting for transfers between devices, device_fn(): lax.ppermute((dx_moe + sh_dx).astype(jnp.bfloat16), 'stage', back_perm)  29.6 us
    scatter-add x1, other arithmetic, device_fn(): jax.ops.segment_sum(dx_rows, row_of_pair, num_segments=n_slot)  23.9 us
  transfers between devices with their start and end apart: 10, of which 3 were waited for; matrix products, arithmetic and copies ran while one was open for 45% of the time, Pallas kernels for 14%

commit v1 on v0

v1 whole, which is shorter than its diff:
```python
import functools

import jax
import jax.numpy as jnp
from jax import lax
from jax.experimental import pallas as pl
from jax.experimental.pallas import tpu as pltpu
from jax.sharding import PartitionSpec as P

BF16 = jnp.bfloat16
F32 = jnp.float32
MESH = pl.DeviceIdType.MESH
ALIGN = 16
TILE = 128
VMEM_BYTES = 66_000_000


def dot(lhs, rhs, lhs_dim=1, rhs_dim=0):
    return lax.dot_general(lhs, rhs, (((lhs_dim,), (rhs_dim,)), ((), ())), preferred_element_type=F32)


def onehot(values, axis_iota):
    return jnp.where(values == axis_iota, 1.0, 0.0).astype(BF16)


def flip(me, step):
    out = 0
    for weight in (4, 2, 1):
        mine = (me // weight) % 2
        mask = (step // weight) % 2
        out = out + weight * (mine + mask - 2 * mine * mask)
    return out


def greet_all(n_stage, n_group):
    stage, me = lax.axis_index('stage'), lax.axis_index('expert')
    barrier = pltpu.get_barrier_semaphore()
    for ds in range(n_stage):
        for dk in range(n_group):
            if ds or dk:
                pl.semaphore_signal(barrier, inc=1, device_id=((stage + ds) % n_stage, (me + dk) % n_group), device_id_type=MESH)
    pl.semaphore_wait(barrier, n_stage * n_group - 1)


def dispatch_kernel(n_local, n_rows, x_hbm, dy_hbm, ordx_ref, ordy_ref, meta_ref, xs_hbm, dys_hbm, gate_ref, pos_ref, bounds_ref,
                    x_v, dy_v, xp, dyp, xr, dyr, meta_r, xs, dys,
                    load_sem, xs_send, xs_recv, dy_send, dy_recv, m_send, m_recv, out_sem):
    stage, me = lax.axis_index('stage'), lax.axis_index('expert')
    n_group, cap = xr.shape[0], xr.shape[1]
    n_tok = x_v.shape[0]
    n_pos = n_rows - TILE
    load_x = pltpu.make_async_copy(x_hbm, x_v, load_sem.at[0])
    load_dy = pltpu.make_async_copy(dy_hbm, dy_v, load_sem.at[1])
    load_x.start()
    load_dy.start()
    greet_all(2, n_group)

    def meta_copy(step):
        peer = flip(me, step)
        return pltpu.make_async_remote_copy(src_ref=meta_ref.at[peer], dst_ref=meta_r.at[step], send_sem=m_send.at[step],
                                            recv_sem=m_recv.at[step], device_id=(1 - stage, peer), device_id_type=MESH)

    def x_copy(step):
        return pltpu.make_async_remote_copy(src_ref=xp.at[step], dst_ref=xr.at[step], send_sem=xs_send.at[step],
                                            recv_sem=xs_recv.at[step], device_id=(1 - stage, flip(me, step)), device_id_type=MESH)

    def dy_copy(step):
        return pltpu.make_async_remote_copy(src_ref=dyp.at[step], dst_ref=dyr.at[step], send_sem=dy_send.at[step],
                                            recv_sem=dy_recv.at[step], device_id=(stage, flip(me, step)), device_id_type=MESH)

    for step in range(n_group):
        meta_copy(step).start()
    load_x.wait()
    load_dy.wait()

    def send_step(step, carry):
        peer = flip(me, step)
        rows = pl.ds(pl.multiple_of(peer * cap, cap), cap)
        lanes = lax.broadcasted_iota(jnp.int32, (cap, n_tok), 1)
        xp[step] = dot(onehot(ordx_ref[rows, :], lanes), x_v[...]).astype(BF16)
        block = dot(onehot(ordy_ref[rows, :], lanes), dy_v[...]).astype(BF16)
        x_copy(step).start()

        @pl.when(step == 0)
        def _():
            dyr[0] = block

        @pl.when(step > 0)
        def _():
            dyp[step] = block
            dy_copy(step).start()
        return carry

    lax.fori_loop(0, n_group, send_step, 0)

    for ref in (xs, dys):
        ref[...] = jnp.zeros(ref.shape, BF16)
    gate_ref[...] = jnp.zeros(gate_ref.shape, F32)

    for step in range(n_group):
        meta_copy(step).wait()
    sub = lax.broadcasted_iota(jnp.int32, (n_local, cap), 0).astype(F32)
    hits = [jnp.where(meta_r[step, 0:1, :] == sub, 1.0, 0.0) for step in range(n_group)]
    counts = [jnp.sum(hit, axis=1, keepdims=True) for hit in hits]
    total = sum(counts[1:], counts[0])
    units = jnp.floor((total + (ALIGN - 1)) * (1.0 / ALIGN))
    lower = jnp.where(lax.broadcasted_iota(jnp.int32, (n_local, n_local), 1) < lax.broadcasted_iota(jnp.int32, (n_local, n_local), 0), 1.0, 0.0)
    first = dot(lower.astype(BF16), jnp.broadcast_to(units, (n_local, TILE)).astype(BF16)) * float(ALIGN)
    bounds_ref[0] = first.astype(jnp.int32)
    bounds_ref[1] = jnp.broadcast_to(total, (n_local, TILE)).astype(jnp.int32)
    earlier = jnp.where(lax.broadcasted_iota(jnp.int32, (cap, cap), 0) < lax.broadcasted_iota(jnp.int32, (cap, cap), 1), 1.0, 0.0).astype(BF16)
    base = first[:, 0:1]
    for step in range(n_group):
        rank = dot(hits[step].astype(BF16), earlier) + base
        pos_ref[step] = jnp.sum(hits[step] * rank, axis=0, keepdims=True).astype(jnp.int32)
        base = base + counts[step]

    def merge_step(step, carry):
        pos = pos_ref[step]
        gate = meta_r[step, 1:2, :]
        x_copy(step).wait()

        @pl.when(step > 0)
        def _():
            dy_copy(step).wait()

        def merge_rows(blk, inner):
            rows = pl.ds(pl.multiple_of(blk * cap, cap), cap)
            match = pos == lax.broadcasted_iota(jnp.int32, (cap, cap), 0) + blk * cap
            place = jnp.where(match, 1.0, 0.0).astype(BF16)
            xs[rows, :] += dot(place, xr[step]).astype(BF16)
            dys[rows, :] += dot(place, dyr[step]).astype(BF16)
            gate_ref[rows, :] += jnp.sum(jnp.where(match, gate, 0.0), axis=1, keepdims=True)
            return inner

        return lax.fori_loop(0, n_pos // cap, merge_rows, carry)

    lax.fori_loop(0, n_group, merge_step, 0)
    out_x = pltpu.make_async_copy(xs, xs_hbm, out_sem.at[0])
    out_dy = pltpu.make_async_copy(dys, dys_hbm, out_sem.at[1])
    out_x.start()
    out_dy.start()
    out_x.wait()
    out_dy.wait()


def dispatch(x_tok, dy_tok, ordx, ordy, meta, n_local, n_rows):
    n_group, cap = meta.shape[0], meta.shape[2]
    n_tok, width = x_tok.shape
    any_spec = pl.BlockSpec(memory_space=pl.ANY)
    vmem_spec = pl.BlockSpec(memory_space=pltpu.VMEM)
    dma = pltpu.SemaphoreType.DMA
    blocks = pltpu.VMEM((n_group, cap, width), BF16)
    return pl.pallas_call(
        functools.partial(dispatch_kernel, n_local, n_rows),
        out_shape=(jax.ShapeDtypeStruct((n_rows, width), BF16), jax.ShapeDtypeStruct((n_rows, width), BF16),
                   jax.ShapeDtypeStruct((n_rows, 1), F32), jax.ShapeDtypeStruct((n_group, 1, cap), jnp.int32),
                   jax.ShapeDtypeStruct((2, n_local, TILE), jnp.int32)),
        in_specs=[any_spec, any_spec, vmem_spec, vmem_spec, vmem_spec],
        out_specs=(any_spec, any_spec, vmem_spec, vmem_spec, vmem_spec),
        scratch_shapes=[pltpu.VMEM((n_tok, width), BF16), pltpu.VMEM((n_tok, width), BF16), blocks, blocks, blocks, blocks,
                        pltpu.VMEM(meta.shape, F32), pltpu.VMEM((n_rows, width), BF16), pltpu.VMEM((n_rows, width), BF16),
                        dma((2,)), dma((n_group,)), dma((n_group,)), dma((n_group,)), dma((n_group,)), dma((n_group,)), dma((n_group,)),
                        dma((2,))],
        compiler_params=pltpu.CompilerParams(collective_id=0, has_side_effects=True, vmem_limit_bytes=VMEM_BYTES),
        name='dispatch',
    )(x_tok, dy_tok, ordx, ordy, meta)


def swiglu_grads(pre_a, pre_b, grad_hid):
    sig_a = jax.nn.sigmoid(pre_a)
    act_a = pre_a * sig_a
    hidden = (act_a * pre_b).astype(BF16)
    grad_a = (grad_hid * pre_b * sig_a * (1.0 + pre_a * (1.0 - sig_a))).astype(BF16)
    grad_b = (grad_hid * act_a).astype(BF16)
    return hidden, grad_a, grad_b


def expert_kernel(first_ref, count_ref, xs_hbm, dys_hbm, gate_ref, w1, w3, w2, u1, u3, u2,
                  ys_hbm, dxs_hbm, g1, g3, g2, s1_hbm, s3_hbm, s2_hbm,
                  xs, dys, ys, dxs, hs, das, dbs, s1, s3, s2, acc1, acc3, acc2, sem, osem):
    expert = pl.program_id(0)
    n_rows = xs.shape[0]
    n_pos = n_rows - TILE

    @pl.when(expert == 0)
    def _():
        load_x = pltpu.make_async_copy(xs_hbm, xs, sem.at[0])
        load_dy = pltpu.make_async_copy(dys_hbm, dys, sem.at[1])
        load_x.start()
        load_dy.start()
        for ref in (ys, dxs):
            ref[...] = jnp.zeros(ref.shape, BF16)
        for ref in (s1, s3, s2):
            ref[...] = jnp.zeros(ref.shape, F32)
        for ref in (hs, das, dbs):
            ref[pl.ds(n_pos, TILE), :] = jnp.zeros((TILE, ref.shape[1]), BF16)
        load_x.wait()
        load_dy.wait()

        def shared_tile(blk, carry):
            rows = pl.ds(pl.multiple_of(blk * 2 * TILE, 2 * TILE), 2 * TILE)
            x_blk, dy_blk = xs[rows, :], dys[rows, :]
            hidden, grad_a, grad_b = swiglu_grads(dot(x_blk, u1[...]), dot(x_blk, u3[...]), dot(dy_blk, u2[...], 1, 1))
            hs[rows, :] = hidden
            das[rows, :] = grad_a
            dbs[rows, :] = grad_b
            s1[...] += dot(x_blk, grad_a, 0, 0)
            s3[...] += dot(x_blk, grad_b, 0, 0)
            s2[...] += dot(hidden, dy_blk, 0, 0)
            return carry

        lax.fori_loop(0, n_pos // (2 * TILE), shared_tile, 0)
        for k, (src, dst) in enumerate(((s1, s1_hbm), (s3, s3_hbm), (s2, s2_hbm))):
            pltpu.make_async_copy(src, dst, osem.at[k]).start()

    for ref in (acc1, acc3, acc2):
        ref[...] = jnp.zeros(ref.shape, F32)
    first, count = first_ref[expert], count_ref[expert]

    def tile_step(tile, carry):
        rows = pl.ds(pl.multiple_of(first + tile * TILE, ALIGN), TILE)
        x_blk, dy_blk, gate = xs[rows, :], dys[rows, :], gate_ref[rows, :]
        live = lax.broadcasted_iota(jnp.int32, (TILE, 1), 0) + tile * TILE < count
        grad_out = jnp.where(live, gate * dy_blk.astype(F32), 0.0).astype(BF16)
        hidden, grad_a, grad_b = swiglu_grads(dot(x_blk, w1[0]), dot(x_blk, w3[0]), dot(grad_out, w2[0], 1, 1))
        ys[rows, :] = (gate * dot(hidden, w2[0]) + dot(hs[rows, :], u2[...])).astype(BF16)
        dxs[rows, :] = ((dot(grad_a, w1[0], 1, 1) + dot(grad_b, w3[0], 1, 1))
                        + (dot(das[rows, :], u1[...], 1, 1) + dot(dbs[rows, :], u3[...], 1, 1))).astype(BF16)
        acc1[...] += dot(x_blk, grad_a, 0, 0)
        acc3[...] += dot(x_blk, grad_b, 0, 0)
        acc2[...] += dot(hidden, grad_out, 0, 0)
        return carry

    lax.fori_loop(0, (count + TILE - 1) // TILE, tile_step, 0)
    g1[0] = acc1[...].astype(BF16)
    g3[0] = acc3[...].astype(BF16)
    g2[0] = acc2[...].astype(BF16)

    @pl.when(expert == pl.num_programs(0) - 1)
    def _():
        out_y = pltpu.make_async_copy(ys, ys_hbm, sem.at[0])
        out_dx = pltpu.make_async_copy(dxs, dxs_hbm, sem.at[1])
        out_y.start()
        out_dx.start()
        for k, (src, dst) in enumerate(((s1, s1_hbm), (s3, s3_hbm), (s2, s2_hbm))):
            pltpu.make_async_copy(src, dst, osem.at[k]).wait()
        out_y.wait()
        out_dx.wait()


def experts(first, count, xs, dys, gate, w1, w3, w2, u1, u3, u2):
    n_rows, width = xs.shape
    n_local, _, ff = w1.shape
    fs = u1.shape[1]
    any_spec = pl.BlockSpec(memory_space=pl.ANY)
    one = dict(pipeline_mode=pl.Buffered(1))
    in_spec = pl.BlockSpec((1, width, ff), lambda e, *_: (e, 0, 0))
    out_spec = pl.BlockSpec((1, ff, width), lambda e, *_: (e, 0, 0))
    grid_spec = pltpu.PrefetchScalarGridSpec(
        num_scalar_prefetch=2, grid=(n_local,),
        in_specs=[any_spec, any_spec, pl.BlockSpec((n_rows, 1), lambda e, *_: (0, 0), **one), in_spec, in_spec, out_spec,
                  pl.BlockSpec((width, fs), lambda e, *_: (0, 0), **one), pl.BlockSpec((width, fs), lambda e, *_: (0, 0), **one),
                  pl.BlockSpec((fs, width), lambda e, *_: (0, 0), **one)],
        out_specs=(any_spec, any_spec, in_spec, in_spec, out_spec, any_spec, any_spec, any_spec),
        scratch_shapes=[pltpu.VMEM((n_rows, width), BF16) for _ in range(4)] + [pltpu.VMEM((n_rows, fs), BF16) for _ in range(3)]
        + [pltpu.VMEM((width, fs), F32), pltpu.VMEM((width, fs), F32), pltpu.VMEM((fs, width), F32)]
        + [pltpu.VMEM((width, ff), F32), pltpu.VMEM((width, ff), F32), pltpu.VMEM((ff, width), F32)]
        + [pltpu.SemaphoreType.DMA((2,)), pltpu.SemaphoreType.DMA((3,))])
    return pl.pallas_call(
        expert_kernel, grid_spec=grid_spec,
        out_shape=(jax.ShapeDtypeStruct((n_rows, width), BF16), jax.ShapeDtypeStruct((n_rows, width), BF16),
                   jax.ShapeDtypeStruct(w1.shape, BF16), jax.ShapeDtypeStruct(w3.shape, BF16), jax.ShapeDtypeStruct(w2.shape, BF16),
                   jax.ShapeDtypeStruct(u1.shape, F32), jax.ShapeDtypeStruct(u3.shape, F32), jax.ShapeDtypeStruct(u2.shape, F32)),
        compiler_params=pltpu.CompilerParams(vmem_limit_bytes=VMEM_BYTES, dimension_semantics=('arbitrary',)),
        name='experts',
    )(first, count, xs, dys, gate, w1, w3, w2, u1, u3, u2)


def return_kernel(ys_hbm, dxs_hbm, pos_ref, ordx_ref, ordy_ref, s1_ref, s3_ref, s2_ref, y_ref, dx_ref, f1, f3, f2,
                  ys, dxs, yp, dxp, yr, dxr, h1, h3, h2, r1, r3, r2, q1, q3, q2,
                  load_sem, y_send, y_recv, dx_send, dx_recv, half_send, half_recv, red_send, red_recv, all_send, all_recv, pair_send, pair_recv):
    stage, me = lax.axis_index('stage'), lax.axis_index('expert')
    n_group, cap = yr.shape[0], yr.shape[1]
    n_tok = y_ref.shape[0]
    n_pos = ys.shape[0]
    n_chip = n_group // 2
    chip, core = me // 2, me % 2
    load_y = pltpu.make_async_copy(ys_hbm.at[pl.ds(0, n_pos)], ys, load_sem.at[0])
    load_dx = pltpu.make_async_copy(dxs_hbm.at[pl.ds(0, n_pos)], dxs, load_sem.at[1])
    load_y.start()
    load_dx.start()
    greet_all(2, n_group)
    parts = ((s1_ref, h1, r1, q1, f1), (s3_ref, h3, r3, q3, f3), (s2_ref, h2, r2, q2, f2))

    def y_copy(step):
        return pltpu.make_async_remote_copy(src_ref=yp.at[step], dst_ref=yr.at[step], send_sem=y_send.at[step],
                                            recv_sem=y_recv.at[step], device_id=(stage, flip(me, step)), device_id_type=MESH)

    def dx_copy(step):
        return pltpu.make_async_remote_copy(src_ref=dxp.at[step], dst_ref=dxr.at[step], send_sem=dx_send.at[step],
                                            recv_sem=dx_recv.at[step], device_id=(1 - stage, flip(me, step)), device_id_type=MESH)

    def half_copy(k):
        src, dst = parts[k][0], parts[k][1]
        n = dst.shape[0]
        return pltpu.make_async_remote_copy(src_ref=src.at[pl.ds(pl.multiple_of((1 - core) * n, n), n)], dst_ref=dst, send_sem=half_send.at[k],
                                            recv_sem=half_recv.at[k], device_id=(stage, flip(me, 1)), device_id_type=MESH)

    def red_copy(k, hop):
        src, dst = parts[k][1], parts[k][2]
        n = dst.shape[1]
        there = flip(me, 2 * hop)
        return pltpu.make_async_remote_copy(src_ref=src.at[pl.ds(pl.multiple_of((there // 2) * n, n), n)], dst_ref=dst.at[hop - 1],
                                            send_sem=red_send.at[3 * k + hop - 1], recv_sem=red_recv.at[3 * k + hop - 1],
                                            device_id=(stage, there), device_id_type=MESH)

    def all_copy(k, hop, landing):
        own, full = parts[k][3], parts[k][4]
        n = own.shape[0]
        there = flip(me, 2 * hop)
        slot = (n_chip * core + (there // 2 if landing else chip)) * n
        return pltpu.make_async_remote_copy(src_ref=own, dst_ref=full.at[pl.ds(pl.multiple_of(slot, n), n)],
                                            send_sem=all_send.at[3 * k + hop - 1], recv_sem=all_recv.at[3 * k + hop - 1],
                                            device_id=(stage, there), device_id_type=MESH)

    def pair_copy(k, landing):
        full = parts[k][4]
        n = full.shape[0] // 2
        rows = pl.ds(pl.multiple_of(((1 - core) if landing else core) * n, n), n)
        return pltpu.make_async_remote_copy(src_ref=full.at[rows], dst_ref=full.at[rows], send_sem=pair_send.at[k],
                                            recv_sem=pair_recv.at[k], device_id=(stage, flip(me, 1)), device_id_type=MESH)

    for k in range(3):
        half_copy(k).start()
    load_y.wait()
    load_dx.wait()

    def send_step(step, carry):
        rows = pl.ds(pl.multiple_of(step * cap, cap), cap)
        pick = onehot(pos_ref[rows, :], lax.broadcasted_iota(jnp.int32, (cap, n_pos), 1))
        dxp[step] = dot(pick, dxs[...]).astype(BF16)
        block = dot(pick, ys[...]).astype(BF16)
        dx_copy(step).start()

        @pl.when(step == 0)
        def _():
            yr[0] = block
            for k in range(3):
                half_copy(k).wait()
            for src, half, _r, _q, _f in parts:
                n = half.shape[0]
                half[...] += src[pl.ds(pl.multiple_of(core * n, n), n), :]

        @pl.when(step > 0)
        def _():
            yp[step] = block
            y_copy(step).start()

        @pl.when(step == 1)
        def _():
            for k in range(3):
                for hop in (1, 2, 3):
                    red_copy(k, hop).start()
        return carry

    lax.fori_loop(0, n_group, send_step, 0)
    y_ref[...] = jnp.zeros(y_ref.shape, BF16)
    dx_ref[...] = jnp.zeros(dx_ref.shape, BF16)

    def home_step(step, carry):
        peer = flip(me, step)

        @pl.when(step > 0)
        def _():
            y_copy(step).wait()
        dx_copy(step).wait()
        ord_y, ord_x = ordy_ref[peer], ordx_ref[peer]

        def home_rows(blk, inner):
            rows = pl.ds(pl.multiple_of(blk * cap, cap), cap)
            tok = lax.broadcasted_iota(jnp.int32, (cap, cap), 0) + blk * cap
            y_ref[rows, :] += dot(onehot(ord_y, tok), yr[step]).astype(BF16)
            dx_ref[rows, :] += dot(onehot(ord_x, tok), dxr[step]).astype(BF16)
            return inner

        lax.fori_loop(0, n_tok // cap, home_rows, 0)

        @pl.when(step == 3)
        def _():
            for k in range(3):
                for hop in (1, 2, 3):
                    red_copy(k, hop).wait()
            for _s, half, recv, own, full in parts:
                n = own.shape[0]
                part = half[pl.ds(pl.multiple_of(chip * n, n), n), :] + recv[0] + recv[1] + recv[2]
                own[...] = part.astype(BF16)
                full[pl.ds(pl.multiple_of((n_chip * core + chip) * n, n), n), :] = part.astype(BF16)

        @pl.when(step == 4)
        def _():
            for k in range(3):
                for hop in (1, 2, 3):
                    all_copy(k, hop, False).start()

        @pl.when(step == 6)
        def _():
            for k in range(3):
                for hop in (1, 2, 3):
                    all_copy(k, hop, False).wait_send()
                    all_copy(k, hop, True).wait_recv()
            for k in range(3):
                pair_copy(k, False).start()
        return carry

    lax.fori_loop(0, n_group, home_step, 0)
    for k in range(3):
        pair_copy(k, False).wait_send()
        pair_copy(k, True).wait_recv()


def give_back(ys, dxs, pos, ordx, ordy, s1, s3, s2, n_tok):
    n_group, cap = ordx.shape[0], ordx.shape[2]
    n_rows, width = ys.shape
    n_pos = n_rows - TILE
    any_spec = pl.BlockSpec(memory_space=pl.ANY)
    vmem_spec = pl.BlockSpec(memory_space=pltpu.VMEM)
    dma = pltpu.SemaphoreType.DMA
    blocks = pltpu.VMEM((n_group, cap, width), BF16)
    grads = (s1, s3, s2)
    halves = [pltpu.VMEM((g.shape[0] // 2, g.shape[1]), F32) for g in grads]
    recvs = [pltpu.VMEM((3, g.shape[0] // n_group, g.shape[1]), F32) for g in grads]
    owns = [pltpu.VMEM((g.shape[0] // n_group, g.shape[1]), BF16) for g in grads]
    return pl.pallas_call(
        return_kernel,
        out_shape=(jax.ShapeDtypeStruct((n_tok, width), BF16), jax.ShapeDtypeStruct((n_tok, width), BF16),
                   *[jax.ShapeDtypeStruct(g.shape, BF16) for g in grads]),
        in_specs=[any_spec, any_spec] + [vmem_spec] * 6,
        out_specs=(vmem_spec,) * 5,
        scratch_shapes=[pltpu.VMEM((n_pos, width), BF16), pltpu.VMEM((n_pos, width), BF16), blocks, blocks, blocks, blocks]
        + halves + recvs + owns
        + [dma((2,)), dma((n_group,)), dma((n_group,)), dma((n_group,)), dma((n_group,)), dma((3,)), dma((3,)),
           dma((9,)), dma((9,)), dma((9,)), dma((9,)), dma((3,)), dma((3,))],
        compiler_params=pltpu.CompilerParams(collective_id=1, has_side_effects=True, vmem_limit_bytes=VMEM_BYTES),
        name='give_back',
    )(ys, dxs, pos, ordx, ordy, s1, s3, s2)


def solution(mesh):
    n_stage = mesh.shape['stage']
    n_group = mesh.shape['expert']
    fwd_perm = [(src, (src + 1) % n_stage) for src in range(n_stage)]
    tok_spec = P('stage', 'expert', None)
    w_spec = P('stage', 'expert', None, None)
    sh_spec = P('stage', None, None)

    def device_fn(x_act, route_idx, route_gate, w_in1, w_in3, w_out, ws_in1, ws_in3, ws_out, dy_out):
        n_tok = x_act.shape[1]
        n_local = w_in1.shape[1]
        cap = n_tok // n_group
        n_rows = n_tok + n_local * ALIGN + TILE
        idx = route_idx[0].reshape(n_tok)
        tok_ids = jnp.arange(n_tok, dtype=jnp.int32)
        sorted_idx, order, sorted_gate = lax.sort((idx, tok_ids, route_gate[0].reshape(n_tok)), num_keys=1)
        order_back = lax.ppermute(order, 'stage', fwd_perm)
        lid = (sorted_idx % n_local).astype(F32).reshape(n_group, 1, cap)
        meta = jnp.concatenate([lid, sorted_gate.reshape(n_group, 1, cap), jnp.zeros((n_group, 6, cap), F32)], axis=1)
        xs, dys, gate, pos, bounds = dispatch(x_act[0], dy_out[0], order[:, None], order_back[:, None], meta, n_local, n_rows)
        ys, dxs, g1, g3, g2, s1, s3, s2 = experts(bounds[0, :, 0], bounds[1, :, 0], xs, dys, gate,
                                                  w_in1[0], w_in3[0], w_out[0], ws_in1[0], ws_in3[0], ws_out[0])
        y_tok, dx_tok, f1, f3, f2 = give_back(ys, dxs, pos.reshape(n_tok, 1), order.reshape(n_group, 1, cap),
                                              order_back.reshape(n_group, 1, cap), s1, s3, s2, n_tok)
        return (y_tok[None], dx_tok[None], g1[None], g3[None], g2[None], f1[None], f3[None], f2[None])

    return jax.shard_map(device_fn, mesh=mesh,
                         in_specs=(tok_spec, tok_spec, tok_spec, w_spec, w_spec, w_spec, sh_spec, sh_spec, sh_spec, tok_spec),
                         out_specs=(tok_spec, tok_spec, w_spec, w_spec, w_spec, sh_spec, sh_spec, sh_spec),
                         check_vma=False)
```

time: 926 us -> 433 us (0.47); the launches traced: 911 us -> 432 us
  local copies, waits for them, and re-layouts: 236 us -> 15.8 us
  Pallas kernels: 224 us -> 406 us
  other arithmetic: 169 us -> 5.97 us
  blocking collectives: 117 us -> 0 us
  waiting for transfers between devices: 68.8 us -> 0.01 us
  matrix products: 59 us -> 0 us
  starting transfers between devices: 34.4 us -> 3.35 us
    pallas_call x0 -> x3, Pallas kernels: none -> 406 us  [the longest x1 171 us: give_back(): pl.pallas_call(return_kernel, out_shape=(jax.ShapeDtypeStruct((n_tok, wid...]
    another operation x6 -> x0, Pallas kernels: 149 us -> none
    psum x1 -> x0, blocking collectives: 117 us -> none  [device_fn(): gs_one = lax.psum(gs_one, 'expert')]
    gather x12 -> x0, local copies, waits for them, and re-layouts: 114 us -> none  [the longest x1 13.7 us: device_fn(): recv_dy = lax.all_to_all(dy_tok[safe_tok], 'expert', 0, 0, tiled=True)]
    scatter-add x5 -> x0, other arithmetic: 107 us -> none  [the longest x1 23.9 us: device_fn(): jax.ops.segment_sum(dx_rows, row_of_pair, num_segments=n_slot)]
    unnamed x5 -> x0, Pallas kernels: 75.8 us -> none
    scatter x1 -> x0, local copies, waits for them, and re-layouts: 60.3 us -> none  [device_fn(): jnp.full((n_slot + 1,), n_tok, jnp.int32).at[flat_slot.reshape(-1)]]
    dot_general x9 -> x0, matrix products: 59 us -> none  [the longest x1 10.8 us: shared_pass(): jnp.einsum('tf,df->td', grad_b, w_three, preferred_element_type=jnp.float32)]
  transfers between devices with their start and end apart: 10 -> 1, of which waited for: 3 -> 0; matrix products, arithmetic and copies ran while one was open for 45% -> 0% of each run, Pallas kernels for 14% -> 0%
where the time goes in v1:
time: 433 us; the launch traced here: 432 us
  Pallas kernels  406 us (94%)
  local copies, waits for them, and re-layouts  15.8 us (4%)
  other arithmetic  5.97 us (1%)
    pallas_call x1, Pallas kernels, give_back(): pl.pallas_call(return_kernel, out_shape=(jax.ShapeDtypeStruct((n_tok, wid...  171 us
    pallas_call x1, Pallas kernels, dispatch(): pl.pallas_call(functools.partial(dispatch_kernel, n_local, n_rows), out_s...  137 us
    pallas_call x1, Pallas kernels, experts(): pl.pallas_call(expert_kernel, grid_spec=grid_spec, out_shape=(jax.ShapeDt...  98.5 us
    unnamed x17, local copies, waits for them, and re-layouts  9.62 us
  transfers between devices with their start and end apart: 1, of which 0 were waited for; matrix products, arithmetic and copies ran while one was open for 0% of the time, Pallas kernels for 0%

profile of v1, /device:TPU:0, one launch (start us, length us, event | category | flops | bytes accessed | tf_op | source)
XLA Modules:
  0.0 432.0 jit_solution(6853325035264776600)
XLA Ops:
  0.6 5.3 %sort.21 = (s32[2048]{0:T(1024)S(1)}, s32[2048]{0:T(1024)S(1)}, f32[2048]{0:T(1024)S(1)}) sort(s32[2048]{0:T(1024)} %bitcast.44, s32[2048]{0:T(1024)S(1)} %iota.3, f32[2048]{0:T(1024)} %bitcast.45), dimensions={0}, to_apply=%region_0.0 | sort | flops 22528 | bytes 49152 | tf_op jit(solution)/shard_map/sort | solution.py:464
  5.9 0.0 copy-start.4
  5.9 3.3 collective-permute-start
  9.3 0.1 pad.2.clone
  9.4 0.7 maximum_maximum_fusion.meta_ref
  10.1 1.3 copy.18.ordx_ref
  11.4 0.0 collective-permute-done
  11.4 0.0 copy-start.5
  11.4 1.3 copy.19.ordy_ref
  12.8 136.6 %dispatch.1 = (bf16[2432,1024]{1,0:T(8,128)(2,1)}, bf16[2432,1024]{1,0:T(8,128)(2,1)}, f32[2432,1]{1,0:T(8,128)}, s32[8,1,256]{2,1,0:T(1,128)}, s32[2,16,128]{2,1,0:T(8,128)}) custom-call(bf16[2048,1024]{1,0:T(8,128)(2,1)} %bitcast.28, bf16[2048,1024]{1,0:T(8,128)(2,1)} %bitcast.29, s32[2048,1]{1,0:T(8,128)} %copy.18.ordx_ref, s32[2048,1]{1,0:T(8,128)} %copy.19.ordy_ref, ...), custom_call_target="tpu_custom_call" | custom-call | tf_op jit(solution)/shard_map/dispatch/pallas_call | solution.py:154
  149.4 0.0 copy-done.4
  149.4 0.0 copy-done.5
  149.4 1.4 slice_reduce_fusion
  150.8 2.1 copy.20.pos_ref
  152.8 98.5 %experts.1 = (bf16[2432,1024]{1,0:T(8,128)(2,1)}, bf16[2432,1024]{1,0:T(8,128)(2,1)}, bf16[16,1024,384]{2,1,0:T(8,128)(2,1)}, bf16[16,1024,384]{2,1,0:T(8,128)(2...) custom-call(s32[16]{0:T(128)} %get-tuple-element.51.first_ref, ...), custom_call_target="tpu_custom_call" | custom-call | tf_op jit(solution)/shard_map/experts/pallas_call | solution.py:270
  251.4 171.0 %give_back.1 = (bf16[2048,1024]{1,0:T(8,128)(2,1)}, bf16[2048,1024]{1,0:T(8,128)(2,1)}, bf16[1024,384]{1,0:T(8,128)(2,1)}, bf16[1024,384]{1,0:T(8,128)(2,1)}, bf16[384,1024]{1,0:T(8,128)(2,1)}) custom-call(bf16[2432,1024]{1,0:T(8,128)(2,1)} %get-tuple-element.36.ys_hbm, bf16[2432,1024]{1,0:T(8,128)(2,1)} %get-tuple-element.37.dxs_hbm, ...), custom_call_target="tpu_custom_call" | custom-call | tf_op jit(solution)/shard_map/give_back/pallas_call | solution.py:434
  422.4 0.0 copy-start
  422.4 4.8 %copy.26 = bf16[1,2048,1024]{2,1,0:T(8,128)(2,1)} copy(bf16[1,2048,1024]{2,1,0:T(8,128)(2,1)} %bitcast.31) | data formatting | bytes 8388608
  427.2 0.0 copy-done
  427.2 0.0 copy-start.3
  427.2 0.0 copy-start.2
  427.2 0.0 copy-start.1
  427.2 2.1 copy.27
  429.4 0.0 copy-done.3
  429.4 0.9 copy.28
  430.3 0.0 copy-done.2
  430.3 0.9 copy.29
  431.1 0.0 copy-done.1
  431.1 0.9 copy.30
  (3 shorter events, 0.0 us)
Async XLA Ops:
  5.9 143.5 %copy-start.4 = (s32[2048]{0:T(1024)}, s32[2048]{0:T(1024)S(1)}, u32[]{:S(2)}) copy-start(s32[2048]{0:T(1024)S(1)} %get-tuple-element.29) | copy-start | bytes 24580
  5.9 5.5 %collective-permute-start = (s32[2048]{0:T(1024)S(1)}, s32[2048]{0:T(1024)S(1)}, u32[]{:S(2)}, u32[]{:S(2)}) collective-permute-start(s32[2048]{0:T(1024)S(1)} %get-tuple-element.29), channel_id=1, source_target_pairs={{0,8},{8,0},{1,9},{9,1},{2,10},{10,2},{3,11},{11,3},{4,12},{12,4},... | collective-permute-start | bytes 24584 | tf_op jit(solution)/shard_map/ppermute | solution.py:465
  11.4 138.0 %copy-start.5 = (s32[2048]{0:T(1024)}, s32[2048]{0:T(1024)S(1)}, u32[]{:S(2)}) copy-start(s32[2048]{0:T(1024)S(1)} %collective-permute-done) | copy-start | bytes 24580
  422.4 4.8 %copy-start = (bf16[2048,1024]{1,0:T(8,128)(2,1)S(1)}, bf16[2048,1024]{1,0:T(8,128)(2,1)}, u32[]{:S(2)}) copy-start(bf16[2048,1024]{1,0:T(8,128)(2,1)} %get-tuple-element.43) | copy-start | bytes 12582916
  427.2 2.1 copy-start.3
  427.2 3.0 copy-start.2
  427.2 3.9 copy-start.1

commit v2 on v0

v2 whole, which is shorter than its diff:
```python
import functools

import jax
import jax.numpy as jnp
from jax import lax
from jax.experimental import pallas as pl
from jax.experimental.pallas import tpu as pltpu
from jax.sharding import PartitionSpec as P

BF16 = jnp.bfloat16
F32 = jnp.float32
MESH = pl.DeviceIdType.MESH
ALIGN = 16
TILE = 128
LAG = 2
PLACE = 2
VMEM_BYTES = 66_000_000


def dot(lhs, rhs, lhs_dim=1, rhs_dim=0):
    return lax.dot_general(lhs, rhs, (((lhs_dim,), (rhs_dim,)), ((), ())), preferred_element_type=F32)


def onehot(values, axis_iota):
    return jnp.where(values == axis_iota, 1.0, 0.0).astype(BF16)


def as_column(row):
    return jnp.broadcast_to(row, (TILE, row.shape[1])).T[:, 0:1]


def gate_parts(gate):
    high = gate.astype(BF16).astype(F32)
    middle = (gate - high).astype(BF16).astype(F32)
    low = gate - high - middle
    lane = lax.broadcasted_iota(jnp.int32, (gate.shape[0], TILE), 1)
    return jnp.where(lane == 0, high, jnp.where(lane == 1, middle, jnp.where(lane == 2, low, 0.0))).astype(BF16)


def flip(me, step):
    out = 0
    for weight in (4, 2, 1):
        mine = (me // weight) % 2
        mask = (step // weight) % 2
        out = out + weight * (mine + mask - 2 * mine * mask)
    return out


def stage_order(turn):
    pair, odd = turn // 2, turn % 2
    middle = ((pair + 1) // 2) % 2
    return middle * (1 + pair + 2 * odd) + (1 - middle) * (6 * (pair // 3) + odd)


def plane_order(turn):
    pair, odd = turn // 2, turn % 2
    opening = 1 - (pair + 1) // 2
    return opening * (6 + odd) + (1 - opening) * (3 + pair - 2 * odd)


def greet_all(n_stage, n_group):
    stage, me = lax.axis_index('stage'), lax.axis_index('expert')
    barrier = pltpu.get_barrier_semaphore()
    for ds in range(n_stage):
        for dk in range(n_group):
            if ds or dk:
                pl.semaphore_signal(barrier, inc=1, device_id=((stage + ds) % n_stage, (me + dk) % n_group), device_id_type=MESH)
    pl.semaphore_wait(barrier, n_stage * n_group - 1)


def swiglu_grads(pre, grad_hid):
    ff = grad_hid.shape[1]
    pre_a, pre_b = pre[:, :ff], pre[:, ff:]
    sig_a = jax.nn.sigmoid(pre_a)
    act_a = pre_a * sig_a
    hidden = (act_a * pre_b).astype(BF16)
    grad_a = (grad_hid * pre_b * sig_a * (1.0 + pre_a * (1.0 - sig_a))).astype(BF16)
    grad_b = (grad_hid * act_a).astype(BF16)
    return hidden, jnp.concatenate([grad_a, grad_b], axis=1)


def dispatch_kernel(n_local, n_rows, x_hbm, dy_hbm, ordx_ref, meta_ref, u1_hbm, u3_hbm, u2_hbm,
                    xs_hbm, dys_hbm, hdd_hbm, pos_ref, bounds_ref, ordz, p0, p1, p2, p3,
                    x_v, dy_v, xp, dyp, xr, dyr, meta_r, xs, dys, hdd, hddk, u13, u2, grads, half,
                    load_sem, xs_send, xs_recv, dy_send, dy_recv, m_send, m_recv, z_send, z_recv, h_send, h_recv, out_sem):
    stage, me = lax.axis_index('stage'), lax.axis_index('expert')
    chip, core = me // 2, me % 2
    n_group, cap = xr.shape[0], xr.shape[1]
    n_tok = x_v.shape[0]
    n_pos = n_rows - TILE
    ff = u2.shape[0]
    loads = [pltpu.make_async_copy(src, dst, load_sem.at[k]) for k, (src, dst) in enumerate((
        (x_hbm, x_v), (dy_hbm, dy_v), (u1_hbm, u13.at[:, pl.ds(0, ff)]), (u3_hbm, u13.at[:, pl.ds(ff, ff)]), (u2_hbm, u2)))]
    for load in loads:
        load.start()
    greet_all(2, n_group)

    def meta_copy(step):
        peer = flip(me, step)
        return pltpu.make_async_remote_copy(src_ref=meta_ref.at[peer], dst_ref=meta_r.at[step], send_sem=m_send.at[step],
                                            recv_sem=m_recv.at[step], device_id=(1 - stage, peer), device_id_type=MESH)

    def x_copy(step):
        return pltpu.make_async_remote_copy(src_ref=xp.at[step], dst_ref=xr.at[step], send_sem=xs_send.at[step],
                                            recv_sem=xs_recv.at[step], device_id=(1 - stage, flip(me, step)), device_id_type=MESH)

    def dy_copy(step):
        return pltpu.make_async_remote_copy(src_ref=dyp.at[step], dst_ref=dyr.at[step], send_sem=dy_send.at[step],
                                            recv_sem=dy_recv.at[step], device_id=(stage, flip(me, step)), device_id_type=MESH)

    def half_copy():
        n = half.shape[0]
        return pltpu.make_async_remote_copy(src_ref=grads.at[pl.ds(pl.multiple_of((1 - core) * n, n), n)], dst_ref=half, send_sem=h_send,
                                            recv_sem=h_recv, device_id=(stage, flip(me, 1)), device_id_type=MESH)

    def order_copy():
        return pltpu.make_async_remote_copy(src_ref=ordx_ref, dst_ref=ordz, send_sem=z_send, recv_sem=z_recv,
                                            device_id=(1 - stage, me), device_id_type=MESH)

    order_copy().start()
    for step in range(n_group):
        meta_copy(step).start()
    loads[0].wait()

    def permuted(order, src):
        return dot(onehot(as_column(order), lax.broadcasted_iota(jnp.int32, (cap, n_tok), 1)), src[...]).astype(BF16)

    def send_step(turn):
        step = stage_order(turn)
        xp[step] = permuted(ordx_ref[flip(me, step)], x_v)
        x_copy(step).start()

        @pl.when(turn == 0)
        def _():
            loads[1].wait()
            order_copy().wait()

        @pl.when(turn < 6)
        def _():
            plane = plane_order(turn)
            dyp[plane] = permuted(ordz[flip(me, plane)], dy_v)
            dy_copy(plane).start()

        @pl.when(turn < 2)
        def _():
            block = permuted(ordz[flip(me, turn)], dy_v)

            @pl.when(turn == 0)
            def _():
                dyr[0] = block

            @pl.when(turn == 1)
            def _():
                dyp[1] = block
                dy_copy(1).start()

    def place_rows(step, ref, block):
        pos = pos_ref[step]
        n = n_pos // PLACE

        def place_tile(blk, carry):
            rows = pl.ds(pl.multiple_of(blk * n, n), n)
            place = onehot(pos, lax.broadcasted_iota(jnp.int32, (n, cap), 0) + blk * n)
            ref[rows, :] += dot(place, block[...]).astype(BF16)
            return carry

        lax.fori_loop(0, PLACE, place_tile, 0)

    def shared_block(step):
        x_blk, dy_blk = xr[step], dyr[step]
        hidden, grad_ab = swiglu_grads(dot(x_blk, u13[...]), dot(dy_blk, u2[...], 1, 1))
        hddk[:, :ff] = hidden
        hddk[:, ff:3 * ff] = grad_ab
        hddk[:, 3 * ff:] = gate_parts(as_column(meta_r[step, 1:2, :]))
        grads[:, :2 * ff] += dot(x_blk, grad_ab, 0, 0)
        grads[:, 2 * ff:] += dot(dy_blk, hidden, 0, 0)
        place_rows(step, hdd, hddk)

    def merge_step(turn):
        @pl.when(turn < 6)
        def _():
            plane = plane_order(turn)
            dy_copy(plane).wait()
            place_rows(plane, dys, dyr.at[plane])

        @pl.when(turn < 2)
        def _():
            @pl.when(turn == 1)
            def _():
                dy_copy(1).wait()
            place_rows(turn, dys, dyr.at[turn])

        step = stage_order(turn)
        x_copy(step).wait()

        def shared_turn(back, carry):
            @pl.when(jnp.where(back == 0, (turn > 2) & (turn < 6), (turn < 2) | (turn > 4)))
            def _():
                shared_block(stage_order(turn - 1 + back))
            return carry

        lax.fori_loop(0, 2, shared_turn, 0)
        place_rows(step, xs, xr.at[step])

    def positions():
        for step in range(n_group):
            meta_copy(step).wait()
        sub = lax.broadcasted_iota(jnp.int32, (n_local, cap), 0).astype(F32)
        hits = [jnp.where(meta_r[step, 0:1, :] == sub, 1.0, 0.0) for step in range(n_group)]
        counts = [jnp.sum(hit, axis=1, keepdims=True) for hit in hits]
        total = sum(counts[1:], counts[0])
        units = jnp.floor((total + (ALIGN - 1)) * (1.0 / ALIGN))
        lower = jnp.where(lax.broadcasted_iota(jnp.int32, (n_local, n_local), 1) < lax.broadcasted_iota(jnp.int32, (n_local, n_local), 0), 1.0, 0.0)
        first = dot(lower.astype(BF16), jnp.broadcast_to(units, (n_local, TILE)).astype(BF16)) * float(ALIGN)
        bounds_ref[0] = first.astype(jnp.int32)
        bounds_ref[1] = jnp.broadcast_to(total, (n_local, TILE)).astype(jnp.int32)
        earlier = jnp.where(lax.broadcasted_iota(jnp.int32, (cap, cap), 0) < lax.broadcasted_iota(jnp.int32, (cap, cap), 1), 1.0, 0.0).astype(BF16)
        base = first[:, 0:1]
        for step in range(n_group):
            rank = dot(hits[step].astype(BF16), earlier) + base
            pos_ref[step] = jnp.sum(hits[step] * rank, axis=0, keepdims=True).astype(jnp.int32)
            base = base + counts[step]

    def both(step, carry):
        @pl.when(step < n_group)
        def _():
            send_step(step)

        @pl.when(step == 1)
        def _():
            for ref in (xs, dys, hdd):
                ref[...] = jnp.zeros(ref.shape, BF16)
            grads[...] = jnp.zeros(grads.shape, F32)
            positions()
            for load in loads[2:]:
                load.wait()

        @pl.when(step >= LAG)
        def _():
            merge_step(step - LAG)

        @pl.when(step == 5 + LAG)
        def _():
            outs[1].start()
        return carry

    outs = [pltpu.make_async_copy(src, dst, out_sem.at[k]) for k, (src, dst) in enumerate(((xs, xs_hbm), (dys, dys_hbm), (hdd, hdd_hbm)))]
    lax.fori_loop(0, n_group + LAG, both, 0)
    half_copy().start()
    outs[0].start()
    outs[2].start()
    half_copy().wait()
    n = p0.shape[0]
    for hop, ref in enumerate((p0, p1, p2, p3)):
        there = flip(me, 2 * hop) // 2
        ref[...] = grads[pl.ds(pl.multiple_of((4 * core + there) * n, n), n), :] + half[pl.ds(pl.multiple_of(there * n, n), n), :]
    for out in outs:
        out.wait()


def dispatch(x_tok, dy_tok, ordx, meta, u1, u3, u2, n_local, n_rows):
    n_group, cap = meta.shape[0], meta.shape[2]
    n_tok, width = x_tok.shape
    ff = u1.shape[1]
    any_spec = pl.BlockSpec(memory_space=pl.ANY)
    vmem_spec = pl.BlockSpec(memory_space=pltpu.VMEM)
    dma = pltpu.SemaphoreType.DMA
    blocks = pltpu.VMEM((n_group, cap, width), BF16)
    part = jax.ShapeDtypeStruct((width // n_group, 3 * ff), F32)
    return pl.pallas_call(
        functools.partial(dispatch_kernel, n_local, n_rows),
        out_shape=(jax.ShapeDtypeStruct((n_rows, width), BF16), jax.ShapeDtypeStruct((n_rows, width), BF16),
                   jax.ShapeDtypeStruct((n_rows, 3 * ff + TILE), BF16), jax.ShapeDtypeStruct((n_group, 1, cap), jnp.int32),
                   jax.ShapeDtypeStruct((2, n_local, TILE), jnp.int32),
                   jax.ShapeDtypeStruct(ordx.shape, jnp.int32), part, part, part, part),
        in_specs=[any_spec, any_spec, vmem_spec, vmem_spec, any_spec, any_spec, any_spec],
        out_specs=(any_spec, any_spec, any_spec) + (vmem_spec,) * 7,
        scratch_shapes=[pltpu.VMEM((n_tok, width), BF16), pltpu.VMEM((n_tok, width), BF16), blocks, blocks, blocks, blocks,
                        pltpu.VMEM(meta.shape, F32), pltpu.VMEM((n_rows, width), BF16), pltpu.VMEM((n_rows, width), BF16),
                        pltpu.VMEM((n_rows, 3 * ff + TILE), BF16), pltpu.VMEM((cap, 3 * ff + TILE), BF16),
                        pltpu.VMEM((width, 2 * ff), BF16), pltpu.VMEM((ff, width), BF16),
                        pltpu.VMEM((width, 3 * ff), F32), pltpu.VMEM((width // 2, 3 * ff), F32),
                        dma((5,)), dma((n_group,)), dma((n_group,)), dma((n_group,)), dma((n_group,)), dma((n_group,)), dma((n_group,)),
                        dma, dma, dma, dma, dma((3,))],
        compiler_params=pltpu.CompilerParams(collective_id=0, has_side_effects=True, vmem_limit_bytes=VMEM_BYTES),
        name='dispatch',
    )(x_tok, dy_tok, ordx, meta, u1, u3, u2)


N_IN = 3
N_CHUNK = 4


def expert_kernel(first_ref, count_ref, xs_hbm, dys_hbm, hdd_hbm, w1, w3, w2, u1_hbm, u3_hbm, u2_hbm,
                  ys_hbm, dxs_hbm, g1, g3, g2,
                  xs, dys, hdd, ys, dxs, u13, u2, w13_v, w2_v, o13, o2, acc13, acc2, sem, rsem, ssem, wsem, osem):
    n_local = w1.shape[0]
    ff = u2.shape[0]
    left, right = pl.ds(0, ff), pl.ds(ff, ff)
    chunk = xs.shape[0] // N_CHUNK
    loads = [pltpu.make_async_copy(src, dst, sem.at[k]) for k, (src, dst) in enumerate((
        (u1_hbm, u13.at[:, left]), (u3_hbm, u13.at[:, right]), (u2_hbm, u2)))]

    def row_loads(part):
        rows = pl.ds(pl.multiple_of(part * chunk, ALIGN), chunk)
        return [pltpu.make_async_copy(src.at[rows], dst.at[rows], rsem.at[part, k])
                for k, (src, dst) in enumerate(((xs_hbm, xs), (dys_hbm, dys), (hdd_hbm, hdd)))]

    def row_stores(part):
        rows = pl.ds(pl.multiple_of(part * chunk, ALIGN), chunk)
        return [pltpu.make_async_copy(src.at[rows], dst.at[rows], ssem.at[part, k]) for k, (src, dst) in enumerate(((ys, ys_hbm), (dxs, dxs_hbm)))]

    def weight_copies(expert):
        slot = lax.rem(expert, N_IN)
        return [pltpu.make_async_copy(w1.at[expert], w13_v.at[slot, :, left], wsem.at[slot, 0]),
                pltpu.make_async_copy(w3.at[expert], w13_v.at[slot, :, right], wsem.at[slot, 1]),
                pltpu.make_async_copy(w2.at[expert], w2_v.at[slot], wsem.at[slot, 2])]

    def grad_copies(expert):
        slot = lax.rem(expert, 2)
        return [pltpu.make_async_copy(o13.at[slot, :, left], g1.at[expert], osem.at[slot, 0]),
                pltpu.make_async_copy(o13.at[slot, :, right], g3.at[expert], osem.at[slot, 1]),
                pltpu.make_async_copy(o2.at[slot], g2.at[expert], osem.at[slot, 2])]

    for copy in row_loads(0) + weight_copies(0) + loads + weight_copies(1):
        copy.start()
    for part in range(1, N_CHUNK):
        for copy in row_loads(part):
            copy.start()
    for copy in weight_copies(2):
        copy.start()
    for ref in (ys, dxs):
        ref[...] = jnp.zeros(ref.shape, BF16)
    for load in loads:
        load.wait()

    def wait_rows(part, carry):
        for copy in row_loads(part):
            copy.wait()
        return carry

    def store_rows(part, carry):
        for copy in row_stores(part):
            copy.start()
        return carry

    def expert_step(expert, carry):
        loaded, stored = carry
        slot, oslot = lax.rem(expert, N_IN), lax.rem(expert, 2)
        for copy in weight_copies(expert):
            copy.wait()

        @pl.when(expert >= 2)
        def _():
            for copy in grad_copies(expert - 2):
                copy.wait()
        first, count = first_ref[expert], count_ref[expert]
        need = (first + jnp.maximum((count + TILE - 1) // TILE, 1) * TILE + chunk - 1) // chunk
        lax.fori_loop(loaded, need, wait_rows, 0)

        def rows_pass(begin, n):
            rows = pl.ds(pl.multiple_of(first + begin, ALIGN), n)
            x_blk, parts = xs[rows, :], hdd[rows, 3 * ff:].astype(F32)
            gate = parts[:, 0:1] + parts[:, 1:2] + parts[:, 2:3]
            live = lax.broadcasted_iota(jnp.int32, (n, 1), 0) + begin < count
            grad_out = jnp.where(live, gate * dys[rows, :].astype(F32), 0.0).astype(BF16)
            hidden, grad_ab = swiglu_grads(dot(x_blk, w13_v[slot]), dot(grad_out, w2_v[slot], 1, 1))
            ys[rows, :] = (gate * dot(hidden, w2_v[slot]) + dot(hdd[rows, :ff], u2[...])).astype(BF16)
            dxs[rows, :] = (dot(grad_ab, w13_v[slot], 1, 1) + dot(hdd[rows, ff:3 * ff], u13[...], 1, 1)).astype(BF16)
            return dot(x_blk, grad_ab, 0, 0), dot(hidden, grad_out, 0, 0)

        for n in (1, 2, 3):
            @pl.when((count > (n - 1) * TILE if n > 1 else count >= 0) & (count <= n * TILE))
            def _():
                grad13, grad2 = rows_pass(0, n * TILE)
                o13[oslot] = grad13.astype(BF16)
                o2[oslot] = grad2.astype(BF16)

        @pl.when(count > 3 * TILE)
        def _():
            acc13[...] = jnp.zeros(acc13.shape, F32)
            acc2[...] = jnp.zeros(acc2.shape, F32)

            def tile_step(tile, inner):
                grad13, grad2 = rows_pass(tile * TILE, TILE)
                acc13[...] += grad13
                acc2[...] += grad2
                return inner

            lax.fori_loop(0, (count + TILE - 1) // TILE, tile_step, 0)
            o13[oslot] = acc13[...].astype(BF16)
            o2[oslot] = acc2[...].astype(BF16)

        for copy in grad_copies(expert):
            copy.start()

        @pl.when(expert + N_IN < n_local)
        def _():
            for copy in weight_copies(expert + N_IN):
                copy.start()
        final = (first + (count + ALIGN - 1) // ALIGN * ALIGN) // chunk
        lax.fori_loop(stored, final, store_rows, 0)
        return jnp.maximum(loaded, need), jnp.maximum(stored, final)

    loaded, stored = lax.fori_loop(0, n_local, expert_step, (0, 0))
    lax.fori_loop(loaded, N_CHUNK, wait_rows, 0)
    lax.fori_loop(stored, N_CHUNK, store_rows, 0)
    for copy in grad_copies(n_local - 2) + grad_copies(n_local - 1):
        copy.wait()
    for part in range(N_CHUNK):
        for copy in row_stores(part):
            copy.wait()


def experts(first, count, xs, dys, hdd, w1, w3, w2, u1, u3, u2):
    n_rows, width = xs.shape
    ff = w1.shape[2]
    any_spec = pl.BlockSpec(memory_space=pl.ANY)
    smem_spec = pl.BlockSpec(memory_space=pltpu.SMEM)
    rows = pltpu.VMEM((n_rows, width), BF16)
    return pl.pallas_call(
        expert_kernel,
        in_specs=[smem_spec, smem_spec, any_spec, any_spec, any_spec] + [any_spec] * 6,
        out_specs=(any_spec,) * 5,
        out_shape=(jax.ShapeDtypeStruct((n_rows, width), BF16), jax.ShapeDtypeStruct((n_rows, width), BF16),
                   jax.ShapeDtypeStruct(w1.shape, BF16), jax.ShapeDtypeStruct(w3.shape, BF16), jax.ShapeDtypeStruct(w2.shape, BF16)),
        scratch_shapes=[rows, rows, pltpu.VMEM(hdd.shape, BF16), rows, rows,
                        pltpu.VMEM((width, 2 * ff), BF16), pltpu.VMEM((ff, width), BF16),
                        pltpu.VMEM((N_IN, width, 2 * ff), BF16), pltpu.VMEM((N_IN, ff, width), BF16),
                        pltpu.VMEM((2, width, 2 * ff), BF16), pltpu.VMEM((2, ff, width), BF16),
                        pltpu.VMEM((width, 2 * ff), F32), pltpu.VMEM((ff, width), F32),
                        pltpu.SemaphoreType.DMA((3,)), pltpu.SemaphoreType.DMA((N_CHUNK, 3)), pltpu.SemaphoreType.DMA((N_CHUNK, 2)),
                        pltpu.SemaphoreType.DMA((N_IN, 3)), pltpu.SemaphoreType.DMA((2, 3))],
        compiler_params=pltpu.CompilerParams(vmem_limit_bytes=VMEM_BYTES),
        cost_estimate=pl.CostEstimate(flops=40_000_000_000, bytes_accessed=100_000_000, transcendentals=0),
        name='experts',
    )(first, count, xs, dys, hdd, w1, w3, w2, u1, u3, u2)


def return_kernel(ys_hbm, dxs_hbm, pos_ref, ordx_ref, ordy_ref, p0, r1, r2, r3, y_ref, dx_ref, f1, f3, f2,
                  ys, dxs, yp, dxp, yr, dxr, own, own2, all13, all2,
                  load_sem, y_send, y_recv, dx_send, dx_recv, all_send, all_recv, pair_send, pair_recv):
    stage, me = lax.axis_index('stage'), lax.axis_index('expert')
    n_group, cap = yr.shape[0], yr.shape[1]
    n_tok = y_ref.shape[0]
    n_pos = ys.shape[0]
    n_chip = n_group // 2
    chip, core = me // 2, me % 2
    ff = f1.shape[1]
    n_part = own.shape[0]
    load_y = pltpu.make_async_copy(ys_hbm.at[pl.ds(0, n_pos)], ys, load_sem.at[0])
    load_dx = pltpu.make_async_copy(dxs_hbm.at[pl.ds(0, n_pos)], dxs, load_sem.at[1])
    load_dx.start()
    load_y.start()
    greet_all(2, n_group)

    def y_copy(step):
        return pltpu.make_async_remote_copy(src_ref=yp.at[step], dst_ref=yr.at[step], send_sem=y_send.at[step],
                                            recv_sem=y_recv.at[step], device_id=(stage, flip(me, step)), device_id_type=MESH)

    def dx_copy(step):
        return pltpu.make_async_remote_copy(src_ref=dxp.at[step], dst_ref=dxr.at[step], send_sem=dx_send.at[step],
                                            recv_sem=dx_recv.at[step], device_id=(1 - stage, flip(me, step)), device_id_type=MESH)

    def all_copies(hop, landing):
        there = flip(me, 2 * hop)
        slot = n_chip * core + (there // 2 if landing else chip)
        return [pltpu.make_async_remote_copy(src_ref=src, dst_ref=dst.at[slot], send_sem=all_send.at[2 * hop - 2 + k],
                                             recv_sem=all_recv.at[2 * hop - 2 + k], device_id=(stage, there), device_id_type=MESH)
                for k, (src, dst) in enumerate(((own, all13), (own2, all2)))]

    def pair_copies(landing):
        rows = pl.ds(((1 - core) if landing else core) * n_chip, n_chip)
        return [pltpu.make_async_remote_copy(src_ref=ref.at[rows], dst_ref=ref.at[rows], send_sem=pair_send.at[k],
                                             recv_sem=pair_recv.at[k], device_id=(stage, flip(me, 1)), device_id_type=MESH)
                for k, ref in enumerate((all13, all2))]

    part = p0[...] + r1[...] + r2[...] + r3[...]
    own[...] = part[:, :2 * ff].astype(BF16)
    own2[...] = part[:, 2 * ff:].T.astype(BF16)
    all13[n_chip * core + chip] = part[:, :2 * ff].astype(BF16)
    all2[n_chip * core + chip] = part[:, 2 * ff:].T.astype(BF16)
    load_dx.wait()

    def picked(step, src):
        return dot(onehot(as_column(pos_ref[step]), lax.broadcasted_iota(jnp.int32, (cap, n_pos), 1)), src[...]).astype(BF16)

    def send_step(turn):
        step = stage_order(turn)
        dxp[step] = picked(step, dxs)
        dx_copy(step).start()

        @pl.when(turn == 0)
        def _():
            load_y.wait()

        @pl.when(turn < 6)
        def _():
            plane = plane_order(turn)
            yp[plane] = picked(plane, ys)
            y_copy(plane).start()

        @pl.when(turn < 2)
        def _():
            block = picked(turn, ys)

            @pl.when(turn == 0)
            def _():
                yr[0] = block

            @pl.when(turn == 1)
            def _():
                yp[1] = block
                y_copy(1).start()

    def home_rows(order, ref, block):
        n = n_tok // PLACE

        def home_tile(blk, carry):
            rows = pl.ds(pl.multiple_of(blk * n, n), n)
            tok = lax.broadcasted_iota(jnp.int32, (n, cap), 0) + blk * n
            ref[rows, :] += dot(onehot(order, tok), block[...]).astype(BF16)
            return carry

        lax.fori_loop(0, PLACE, home_tile, 0)

    def home_step(turn):
        @pl.when(turn < 6)
        def _():
            plane = plane_order(turn)
            y_copy(plane).wait()
            home_rows(ordy_ref[flip(me, plane)], y_ref, yr.at[plane])

        @pl.when(turn < 2)
        def _():
            @pl.when(turn == 1)
            def _():
                y_copy(1).wait()
            home_rows(ordy_ref[flip(me, turn)], y_ref, yr.at[turn])

        step = stage_order(turn)
        dx_copy(step).wait()
        home_rows(ordx_ref[flip(me, step)], dx_ref, dxr.at[step])

    def both(step, carry):
        @pl.when(step < n_group)
        def _():
            send_step(step)

        @pl.when(step == 1)
        def _():
            y_ref[...] = jnp.zeros(y_ref.shape, BF16)
            dx_ref[...] = jnp.zeros(dx_ref.shape, BF16)
            for hop in (1, 2, 3):
                for copy in all_copies(hop, False):
                    copy.start()

        @pl.when(step >= LAG)
        def _():
            home_step(step - LAG)

        @pl.when(step == 6)
        def _():
            for hop in (1, 2, 3):
                for copy in all_copies(hop, False):
                    copy.wait_send()
                for copy in all_copies(hop, True):
                    copy.wait_recv()
            for copy in pair_copies(False):
                copy.start()

        @pl.when(step == 8)
        def _():
            for copy in pair_copies(False):
                copy.wait_send()
            for copy in pair_copies(True):
                copy.wait_recv()
            for k in range(n_group):
                rows = pl.ds(k * n_part, n_part)
                f1[rows, :] = all13[k, :, :ff]
                f3[rows, :] = all13[k, :, ff:]
                f2[:, rows] = all2[k]
        return carry

    lax.fori_loop(0, n_group + LAG, both, 0)


def give_back(ys, dxs, pos, ordx, ordy, p0, r1, r2, r3, n_tok):
    n_group, cap = ordx.shape[0], ordx.shape[2]
    n_rows, width = ys.shape
    n_pos = n_rows - TILE
    n_part, ff = p0.shape[0], p0.shape[1] // 3
    any_spec = pl.BlockSpec(memory_space=pl.ANY)
    vmem_spec = pl.BlockSpec(memory_space=pltpu.VMEM)
    dma = pltpu.SemaphoreType.DMA
    blocks = pltpu.VMEM((n_group, cap, width), BF16)
    in_shape = jax.ShapeDtypeStruct((width, ff), BF16)
    return pl.pallas_call(
        return_kernel,
        out_shape=(jax.ShapeDtypeStruct((n_tok, width), BF16), jax.ShapeDtypeStruct((n_tok, width), BF16),
                   in_shape, in_shape, jax.ShapeDtypeStruct((ff, width), BF16)),
        in_specs=[any_spec, any_spec] + [vmem_spec] * 7,
        out_specs=(vmem_spec,) * 5,
        scratch_shapes=[pltpu.VMEM((n_pos, width), BF16), pltpu.VMEM((n_pos, width), BF16), blocks, blocks, blocks, blocks,
                        pltpu.VMEM((n_part, 2 * ff), BF16), pltpu.VMEM((ff, n_part), BF16),
                        pltpu.VMEM((n_group, n_part, 2 * ff), BF16), pltpu.VMEM((n_group, ff, n_part), BF16),
                        dma((2,)), dma((n_group,)), dma((n_group,)), dma((n_group,)), dma((n_group,)),
                        dma((6,)), dma((6,)), dma((2,)), dma((2,))],
        compiler_params=pltpu.CompilerParams(collective_id=1, has_side_effects=True, vmem_limit_bytes=VMEM_BYTES),
        name='give_back',
    )(ys, dxs, pos, ordx, ordy, p0, r1, r2, r3)


def solution(mesh):
    n_group = mesh.shape['expert']
    tok_spec = P('stage', 'expert', None)
    w_spec = P('stage', 'expert', None, None)
    sh_spec = P('stage', None, None)

    def device_fn(x_act, route_idx, route_gate, w_in1, w_in3, w_out, ws_in1, ws_in3, ws_out, dy_out):
        n_tok = x_act.shape[1]
        n_local = w_in1.shape[1]
        cap = n_tok // n_group
        n_rows = n_tok + n_local * ALIGN + TILE
        idx = route_idx[0].reshape(n_tok)
        tok_ids = jnp.arange(n_tok, dtype=jnp.int32)
        sorted_idx, order, sorted_gate = lax.sort((idx, tok_ids, route_gate[0].reshape(n_tok)), num_keys=1)
        order = order.reshape(n_group, 1, cap)
        lid = (sorted_idx % n_local).astype(F32).reshape(n_group, 1, cap)
        meta = jnp.concatenate([lid, sorted_gate.reshape(n_group, 1, cap), jnp.zeros((n_group, 6, cap), F32)], axis=1)
        xs, dys, hdd, pos, bounds, order_back, p0, p1, p2, p3 = dispatch(
            x_act[0], dy_out[0], order, meta, ws_in1[0], ws_in3[0], ws_out[0], n_local, n_rows)
        recv = [lax.ppermute(part, 'expert', [(k, k ^ (2 * hop)) for k in range(n_group)]) for hop, part in ((1, p1), (2, p2), (3, p3))]
        ys, dxs, g1, g3, g2 = experts(bounds[0, :, 0], bounds[1, :, 0], xs, dys, hdd,
                                      w_in1[0], w_in3[0], w_out[0], ws_in1[0], ws_in3[0], ws_out[0])
        y_tok, dx_tok, f1, f3, f2 = give_back(ys, dxs, pos, order, order_back, p0, *recv, n_tok)
        return (y_tok[None], dx_tok[None], g1[None], g3[None], g2[None], f1[None], f3[None], f2[None])

    return jax.shard_map(device_fn, mesh=mesh,
                         in_specs=(tok_spec, tok_spec, tok_spec, w_spec, w_spec, w_spec, sh_spec, sh_spec, sh_spec, tok_spec),
                         out_specs=(tok_spec, tok_spec, w_spec, w_spec, w_spec, sh_spec, sh_spec, sh_spec),
                         check_vma=False)
```

time: 926 us -> 335 us (0.36); the launches traced: 911 us -> 335 us
  local copies, waits for them, and re-layouts: 236 us -> 11.8 us
  other arithmetic: 169 us -> 6.57 us
  blocking collectives: 117 us -> 0 us
  Pallas kernels: 224 us -> 312 us
  waiting for transfers between devices: 68.8 us -> 0.01 us
  matrix products: 59 us -> 0 us
  starting transfers between devices: 34.4 us -> 3.52 us
    pallas_call x0 -> x3, Pallas kernels: none -> 312 us  [the longest x1 129 us: dispatch(): pl.pallas_call(functools.partial(dispatch_kernel, n_local, n_rows), out_s...]
    another operation x6 -> x0, Pallas kernels: 149 us -> none
    psum x1 -> x0, blocking collectives: 117 us -> none  [device_fn(): gs_one = lax.psum(gs_one, 'expert')]
    gather x12 -> x0, local copies, waits for them, and re-layouts: 114 us -> none  [the longest x1 13.7 us: device_fn(): recv_dy = lax.all_to_all(dy_tok[safe_tok], 'expert', 0, 0, tiled=True)]
    scatter-add x5 -> x0, other arithmetic: 107 us -> none  [the longest x1 23.9 us: device_fn(): jax.ops.segment_sum(dx_rows, row_of_pair, num_segments=n_slot)]
    unnamed x5 -> x0, Pallas kernels: 75.8 us -> none
    scatter x1 -> x0, local copies, waits for them, and re-layouts: 60.3 us -> none  [device_fn(): jnp.full((n_slot + 1,), n_tok, jnp.int32).at[flat_slot.reshape(-1)]]
    dot_general x9 -> x0, matrix products: 59 us -> none  [the longest x1 10.8 us: shared_pass(): jnp.einsum('tf,df->td', grad_b, w_three, preferred_element_type=jnp.float32)]
  transfers between devices with their start and end apart: 10 -> 3, of which waited for: 3 -> 0; matrix products, arithmetic and copies ran while one was open for 45% -> 0% of each run, Pallas kernels for 14% -> 18%
where the time goes in v2:
time: 335 us
  Pallas kernels  312 us (93%)
  local copies, waits for them, and re-layouts  11.8 us (4%)
  other arithmetic  6.57 us (2%)
  starting transfers between devices  3.52 us (1%)
    pallas_call x1, Pallas kernels, dispatch(): pl.pallas_call(functools.partial(dispatch_kernel, n_local, n_rows), out_s...  129 us
    pallas_call x1, Pallas kernels, give_back(): pl.pallas_call(return_kernel, out_shape=(jax.ShapeDtypeStruct((n_tok, wid...  122 us
    pallas_call x1, Pallas kernels, experts(): pl.pallas_call(expert_kernel, in_specs=[smem_spec, smem_spec, any_spec, a...  60.7 us
    unnamed x15, local copies, waits for them, and re-layouts  10.4 us
  transfers between devices with their start and end apart: 3, of which 0 were waited for; matrix products, arithmetic and copies ran while one was open for 0% of the time, Pallas kernels for 18%

profile of v2, /device:TPU:0, one launch (start us, length us, event | category | flops | bytes accessed | tf_op | source)
XLA Modules:
  0.0 334.7 jit_solution(12108045487394486039)
XLA Ops:
  0.6 5.9 %sort.21 = (s32[2048]{0:T(1024)S(1)}, s32[2048]{0:T(1024)}, f32[2048]{0:T(1024)S(1)}) sort(s32[2048]{0:T(1024)} %bitcast.37, s32[2048]{0:T(1024)S(1)} %iota.3, f32[2048]{0:T(1024)} %bitcast.38), dimensions={0}, to_apply=%region_0.0 | sort | flops 22528 | bytes 49152 | tf_op jit(solution)/shard_map/sort | solution.py:627
  6.5 0.1 pad.2.clone
  6.6 0.7 maximum_maximum_fusion.meta_ref
  7.3 129.3 %dispatch.1 = (bf16[2432,1024]{1,0:T(8,128)(2,1)}, bf16[2432,1024]{1,0:T(8,128)(2,1)}, bf16[2432,1280]{1,0:T(8,128)(2,1)}, s32[8,1,256]{2,1,0:T(1,128)}, s32[2,1...) custom-call(bf16[2048,1024]{1,0:T(8,128)(2,1)} %bitcast.21, ...), custom_call_target="tpu_custom_call" | custom-call | tf_op jit(solution)/shard_map/dispatch/pallas_call | solution.py:270
  136.6 1.4 collective-permute-start
  138.0 1.5 collective-permute-start.1
  139.5 0.7 collective-permute-start.2
  140.2 1.3 slice_reduce_fusion
  141.5 60.7 %experts.1 = (bf16[2432,1024]{1,0:T(8,128)(2,1)}, bf16[2432,1024]{1,0:T(8,128)(2,1)}, bf16[16,1024,384]{2,1,0:T(8,128)(2,1)}, bf16[16,1024,384]{2,1,0:T(8,128)(2,1)}, bf16[16,384,1024]{2,1,0:T(8,128)(2,1)}) custom-call(s32[16]{0:T(128)} %get-tuple-element.55.first_ref, s32[16]{0:T(128)} %get-tuple-element.54.count_ref, ...), custom_call_target="tpu_custom_call" | custom-call | flops 40000000000 | bytes 100000000 | tf_op jit(solution)/shard_map/experts/pallas_call | solution.py:421
  202.2 0.0 collective-permute-done.r1
  202.2 0.0 copy-start.4
  202.2 0.0 collective-permute-done.1.r2
  202.2 0.0 collective-permute-done.2.r3
  202.3 0.8 copy-done.4
  203.0 122.0 %give_back.1 = (bf16[2048,1024]{1,0:T(8,128)(2,1)}, bf16[2048,1024]{1,0:T(8,128)(2,1)}, bf16[1024,384]{1,0:T(8,128)(2,1)}, bf16[1024,384]{1,0:T(8,128)(2,1)}, bf16[384,1024]{1,0:T(8,128)(2,1)}) custom-call(bf16[2432,1024]{1,0:T(8,128)(2,1)} %get-tuple-element.38.ys_hbm, bf16[2432,1024]{1,0:T(8,128)(2,1)} %get-tuple-element.39.dxs_hbm, ...), custom_call_target="tpu_custom_call" | custom-call | tf_op jit(solution)/shard_map/give_back/pallas_call | solution.py:598
  325.1 0.0 copy-start
  325.1 4.8 %copy.23 = bf16[1,2048,1024]{2,1,0:T(8,128)(2,1)} copy(bf16[1,2048,1024]{2,1,0:T(8,128)(2,1)} %bitcast.24) | data formatting | bytes 8388608
  329.9 0.0 copy-done
  329.9 0.0 copy-start.3
  329.9 0.0 copy-start.2
  329.9 0.0 copy-start.1
  329.9 2.1 copy.24
  332.1 0.0 copy-done.3
  332.1 0.9 copy.25
  332.9 0.0 copy-done.2
  332.9 0.9 copy.26
  333.8 0.0 copy-done.1
  333.8 0.9 copy.27
  (3 shorter events, 0.0 us)
Async XLA Ops:
  136.6 65.6 %collective-permute-start = (f32[128,1152]{1,0:T(8,128)}, f32[128,1152]{1,0:T(8,128)S(1)}, u32[]{:S(2)}, u32[]{:S(2)}) collective-permute-start(f32[128,1152]{1,0:T(8,128)} %get-tuple-element.43), channel_id=1, source_target_pairs={{0,2},{1,3},{2,0},{3,1},{4,6},{5,7},{6,4},{7,5},{8,10},{9,11},{10,... | collective-permute-start | bytes 1769480 | tf_op jit(solution)/shard_map/ppermute | solution.py:633
  138.0 64.2 %collective-permute-start.1 = (f32[128,1152]{1,0:T(8,128)}, f32[128,1152]{1,0:T(8,128)}, u32[]{:S(2)}, u32[]{:S(2)}) collective-permute-start(f32[128,1152]{1,0:T(8,128)} %get-tuple-element.44), channel_id=1, source_target_pairs={{0,4},{1,5},{2,6},{3,7},{4,0},{5,1},{6,2},{7,3},{8,12},{9,13},{10,... | collective-permute-start | bytes 1769480 | tf_op jit(solution)/shard_map/ppermute | solution.py:633
  139.5 62.7 %collective-permute-start.2 = (f32[128,1152]{1,0:T(8,128)}, f32[128,1152]{1,0:T(8,128)}, u32[]{:S(2)}, u32[]{:S(2)}) collective-permute-start(f32[128,1152]{1,0:T(8,128)} %get-tuple-element.45), channel_id=1, source_target_pairs={{0,6},{1,7},{2,4},{3,5},{4,2},{5,3},{6,0},{7,1},{8,14},{9,15},{10,... | collective-permute-start | bytes 1769480 | tf_op jit(solution)/shard_map/ppermute | solution.py:633
  202.2 0.8 copy-start.4
  325.1 4.8 %copy-start = (bf16[2048,1024]{1,0:T(8,128)(2,1)S(1)}, bf16[2048,1024]{1,0:T(8,128)(2,1)}, u32[]{:S(2)}) copy-start(bf16[2048,1024]{1,0:T(8,128)(2,1)} %get-tuple-element.47) | copy-start | bytes 12582916
  329.9 2.1 copy-start.3
  329.9 3.0 copy-start.2
  329.9 3.9 %copy-start.1 = (bf16[384,1024]{1,0:T(8,128)(2,1)S(1)}, bf16[384,1024]{1,0:T(8,128)(2,1)}, u32[]{:S(2)}) copy-start(bf16[384,1024]{1,0:T(8,128)(2,1)} %get-tuple-element.53) | copy-start | bytes 2359300

commit v3 on v2

--- a/solution.py
+++ b/solution.py
@@ -12,7 +12,7 @@
 MESH = pl.DeviceIdType.MESH
 ALIGN = 16
 TILE = 128
-LAG = 2
+AHEAD = 2
 PLACE = 2
 VMEM_BYTES = 66_000_000
 
@@ -125,34 +125,13 @@
     def permuted(order, src):
         return dot(onehot(as_column(order), lax.broadcasted_iota(jnp.int32, (cap, n_tok), 1)), src[...]).astype(BF16)
 
-    def send_step(turn):
+    def prepare_x(turn):
         step = stage_order(turn)
         xp[step] = permuted(ordx_ref[flip(me, step)], x_v)
-        x_copy(step).start()
-
-        @pl.when(turn == 0)
-        def _():
-            loads[1].wait()
-            order_copy().wait()
-
-        @pl.when(turn < 6)
-        def _():
-            plane = plane_order(turn)
-            dyp[plane] = permuted(ordz[flip(me, plane)], dy_v)
-            dy_copy(plane).start()
-
-        @pl.when(turn < 2)
-        def _():
-            block = permuted(ordz[flip(me, turn)], dy_v)
-
-            @pl.when(turn == 0)
-            def _():
-                dyr[0] = block
-
-            @pl.when(turn == 1)
-            def _():
-                dyp[1] = block
-                dy_copy(1).start()
+
+    def prepare_dy(turn):
+        plane = plane_order(turn)
+        dyp[plane] = permuted(ordz[flip(me, plane)], dy_v)
 
     def place_rows(step, ref, block):
         pos = pos_ref[step]
@@ -179,9 +158,7 @@
     def merge_step(turn):
         @pl.when(turn < 6)
         def _():
-            plane = plane_order(turn)
-            dy_copy(plane).wait()
-            place_rows(plane, dys, dyr.at[plane])
+            place_rows(plane_order(turn), dys, dyr.at[plane_order(turn)])
 
         @pl.when(turn < 2)
         def _():
@@ -190,9 +167,6 @@
                 dy_copy(1).wait()
             place_rows(turn, dys, dyr.at[turn])
 
-        step = stage_order(turn)
-        x_copy(step).wait()
-
         def shared_turn(back, carry):
             @pl.when(jnp.where(back == 0, (turn > 2) & (turn < 6), (turn < 2) | (turn > 4)))
             def _():
@@ -200,7 +174,7 @@
             return carry
 
         lax.fori_loop(0, 2, shared_turn, 0)
-        place_rows(step, xs, xr.at[step])
+        place_rows(stage_order(turn), xs, xr.at[stage_order(turn)])
 
     def positions():
         for step in range(n_group):
@@ -221,31 +195,74 @@
             pos_ref[step] = jnp.sum(hits[step] * rank, axis=0, keepdims=True).astype(jnp.int32)
             base = base + counts[step]
 
-    def both(step, carry):
-        @pl.when(step < n_group)
-        def _():
-            send_step(step)
-
-        @pl.when(step == 1)
-        def _():
-            for ref in (xs, dys, hdd):
-                ref[...] = jnp.zeros(ref.shape, BF16)
-            grads[...] = jnp.zeros(grads.shape, F32)
-            positions()
-            for load in loads[2:]:
-                load.wait()
-
-        @pl.when(step >= LAG)
-        def _():
-            merge_step(step - LAG)
-
-        @pl.when(step == 5 + LAG)
+    def both(index, carry):
+        turn = index - AHEAD - 1
+        ready = index
+
+        @pl.when(turn >= 0)
+        def _():
+            x_copy(stage_order(turn)).wait()
+
+            @pl.when(turn + AHEAD < n_group)
+            def _():
+                x_copy(stage_order(turn + AHEAD)).start()
+
+            @pl.when(turn < 6)
+            def _():
+                dy_copy(plane_order(turn)).wait()
+
+            @pl.when(turn + AHEAD < 6)
+            def _():
+                dy_copy(plane_order(turn + AHEAD)).start()
+            merge_step(turn)
+
+        @pl.when(ready < n_group)
+        def _():
+            prepare_x(ready)
+
+            @pl.when(ready < AHEAD)
+            def _():
+                x_copy(stage_order(ready)).start()
+
+        @pl.when(ready == 0)
+        def _():
+            loads[1].wait()
+            order_copy().wait()
+
+        @pl.when(ready < 6)
+        def _():
+            prepare_dy(ready)
+
+            @pl.when(ready < AHEAD)
+            def _():
+                dy_copy(plane_order(ready)).start()
+
+        @pl.when((ready > 0) & (ready < 3))
+        def _():
+            block = permuted(ordz[flip(me, 2 - ready)], dy_v)
+
+            @pl.when(ready == 1)
+            def _():
+                dyp[1] = block
+                dy_copy(1).start()
+
+            @pl.when(ready == 2)
+            def _():
+                dyr[0] = block
+                for ref in (xs, dys, hdd):
+                    ref[...] = jnp.zeros(ref.shape, BF16)
+                grads[...] = jnp.zeros(grads.shape, F32)
+                positions()
+                for load in loads[2:]:
+                    load.wait()
+
+        @pl.when(turn == 5)
         def _():
             outs[1].start()
         return carry
 
     outs = [pltpu.make_async_copy(src, dst, out_sem.at[k]) for k, (src, dst) in enumerate(((xs, xs_hbm), (dys, dys_hbm), (hdd, hdd_hbm)))]
-    lax.fori_loop(0, n_group + LAG, both, 0)
+    lax.fori_loop(0, n_group + AHEAD + 1, both, 0)
     half_copy().start()
     outs[0].start()
     outs[2].start()
@@ -291,7 +308,7 @@
 N_CHUNK = 4
 
 
-def expert_kernel(first_ref, count_ref, xs_hbm, dys_hbm, hdd_hbm, w1, w3, w2, u1_hbm, u3_hbm, u2_hbm,
+def expert_kernel(bounds_ref, xs_hbm, dys_hbm, hdd_hbm, w1, w3, w2, u1_hbm, u3_hbm, u2_hbm,
                   ys_hbm, dxs_hbm, g1, g3, g2,
                   xs, dys, hdd, ys, dxs, u13, u2, w13_v, w2_v, o13, o2, acc13, acc2, sem, rsem, ssem, wsem, osem):
     n_local = w1.shape[0]
@@ -354,7 +371,7 @@
         def _():
             for copy in grad_copies(expert - 2):
                 copy.wait()
-        first, count = first_ref[expert], count_ref[expert]
+        first, count = bounds_ref[0, expert, 0], bounds_ref[1, expert, 0]
         need = (first + jnp.maximum((count + TILE - 1) // TILE, 1) * TILE + chunk - 1) // chunk
         lax.fori_loop(loaded, need, wait_rows, 0)
 
@@ -412,7 +429,7 @@
             copy.wait()
 
 
-def experts(first, count, xs, dys, hdd, w1, w3, w2, u1, u3, u2):
+def experts(bounds, xs, dys, hdd, w1, w3, w2, u1, u3, u2):
     n_rows, width = xs.shape
     ff = w1.shape[2]
     any_spec = pl.BlockSpec(memory_space=pl.ANY)
@@ -420,7 +437,7 @@
     rows = pltpu.VMEM((n_rows, width), BF16)
     return pl.pallas_call(
         expert_kernel,
-        in_specs=[smem_spec, smem_spec, any_spec, any_spec, any_spec] + [any_spec] * 6,
+        in_specs=[smem_spec, any_spec, any_spec, any_spec] + [any_spec] * 6,
         out_specs=(any_spec,) * 5,
         out_shape=(jax.ShapeDtypeStruct((n_rows, width), BF16), jax.ShapeDtypeStruct((n_rows, width), BF16),
                    jax.ShapeDtypeStruct(w1.shape, BF16), jax.ShapeDtypeStruct(w3.shape, BF16), jax.ShapeDtypeStruct(w2.shape, BF16)),
@@ -434,7 +451,7 @@
         compiler_params=pltpu.CompilerParams(vmem_limit_bytes=VMEM_BYTES),
         cost_estimate=pl.CostEstimate(flops=40_000_000_000, bytes_accessed=100_000_000, transcendentals=0),
         name='experts',
-    )(first, count, xs, dys, hdd, w1, w3, w2, u1, u3, u2)
+    )(bounds, xs, dys, hdd, w1, w3, w2, u1, u3, u2)
 
 
 def return_kernel(ys_hbm, dxs_hbm, pos_ref, ordx_ref, ordy_ref, p0, r1, r2, r3, y_ref, dx_ref, f1, f3, f2,
@@ -485,34 +502,6 @@
     def picked(step, src):
         return dot(onehot(as_column(pos_ref[step]), lax.broadcasted_iota(jnp.int32, (cap, n_pos), 1)), src[...]).astype(BF16)
 
-    def send_step(turn):
-        step = stage_order(turn)
-        dxp[step] = picked(step, dxs)
-        dx_copy(step).start()
-
-        @pl.when(turn == 0)
-        def _():
-            load_y.wait()
-
-        @pl.when(turn < 6)
-        def _():
-            plane = plane_order(turn)
-            yp[plane] = picked(plane, ys)
-            y_copy(plane).start()
-
-        @pl.when(turn < 2)
-        def _():
-            block = picked(turn, ys)
-
-            @pl.when(turn == 0)
-            def _():
-                yr[0] = block
-
-            @pl.when(turn == 1)
-            def _():
-                yp[1] = block
-                y_copy(1).start()
-
     def home_rows(order, ref, block):
         n = n_tok // PLACE
 
@@ -524,42 +513,65 @@
 
         lax.fori_loop(0, PLACE, home_tile, 0)
 
-    def home_step(turn):
-        @pl.when(turn < 6)
-        def _():
-            plane = plane_order(turn)
-            y_copy(plane).wait()
-            home_rows(ordy_ref[flip(me, plane)], y_ref, yr.at[plane])
-
-        @pl.when(turn < 2)
-        def _():
-            @pl.when(turn == 1)
-            def _():
-                y_copy(1).wait()
-            home_rows(ordy_ref[flip(me, turn)], y_ref, yr.at[turn])
-
-        step = stage_order(turn)
-        dx_copy(step).wait()
-        home_rows(ordx_ref[flip(me, step)], dx_ref, dxr.at[step])
-
-    def both(step, carry):
-        @pl.when(step < n_group)
-        def _():
-            send_step(step)
-
-        @pl.when(step == 1)
-        def _():
-            y_ref[...] = jnp.zeros(y_ref.shape, BF16)
-            dx_ref[...] = jnp.zeros(dx_ref.shape, BF16)
-            for hop in (1, 2, 3):
-                for copy in all_copies(hop, False):
-                    copy.start()
-
-        @pl.when(step >= LAG)
-        def _():
-            home_step(step - LAG)
-
-        @pl.when(step == 6)
+    def both(index, carry):
+        turn = index - AHEAD - 1
+        ready = index
+
+        @pl.when(turn >= 0)
+        def _():
+            dx_copy(stage_order(turn)).wait()
+
+            @pl.when(turn + AHEAD < n_group)
+            def _():
+                dx_copy(stage_order(turn + AHEAD)).start()
+
+            @pl.when(turn < 6)
+            def _():
+                y_copy(plane_order(turn)).wait()
+
+            @pl.when(turn + AHEAD < 6)
+            def _():
+                y_copy(plane_order(turn + AHEAD)).start()
+
+        @pl.when(ready < n_group)
+        def _():
+            dxp[stage_order(ready)] = picked(stage_order(ready), dxs)
+
+            @pl.when(ready < AHEAD)
+            def _():
+                dx_copy(stage_order(ready)).start()
+
+        @pl.when(ready == 0)
+        def _():
+            load_y.wait()
+
+        @pl.when(ready < 6)
+        def _():
+            yp[plane_order(ready)] = picked(plane_order(ready), ys)
+
+            @pl.when(ready < AHEAD)
+            def _():
+                y_copy(plane_order(ready)).start()
+
+        @pl.when((ready > 0) & (ready < 3))
+        def _():
+            block = picked(2 - ready, ys)
+
+            @pl.when(ready == 1)
+            def _():
+                yp[1] = block
+                y_copy(1).start()
+
+            @pl.when(ready == 2)
+            def _():
+                yr[0] = block
+                y_ref[...] = jnp.zeros(y_ref.shape, BF16)
+                dx_ref[...] = jnp.zeros(dx_ref.shape, BF16)
+                for hop in (1, 2, 3):
+                    for copy in all_copies(hop, False):
+                        copy.start()
+
+        @pl.when(turn == 6)
         def _():
             for hop in (1, 2, 3):
                 for copy in all_copies(hop, False):
@@ -569,7 +581,7 @@
             for copy in pair_copies(False):
                 copy.start()
 
-        @pl.when(step == 8)
+        @pl.when(turn == 7)
         def _():
             for copy in pair_copies(False):
                 copy.wait_send()
@@ -580,9 +592,25 @@
                 f1[rows, :] = all13[k, :, :ff]
                 f3[rows, :] = all13[k, :, ff:]
                 f2[:, rows] = all2[k]
+
+        @pl.when((turn == 1) | (turn == 2))
+        def _():
+            step = 2 - turn
+
+            @pl.when(step == 1)
+            def _():
+                y_copy(1).wait()
+            home_rows(ordy_ref[flip(me, step)], y_ref, yr.at[step])
+
+        @pl.when(turn >= 0)
+        def _():
+            @pl.when(turn < 6)
+            def _():
+                home_rows(ordy_ref[flip(me, plane_order(turn))], y_ref, yr.at[plane_order(turn)])
+            home_rows(ordx_ref[flip(me, stage_order(turn))], dx_ref, dxr.at[stage_order(turn)])
         return carry
 
-    lax.fori_loop(0, n_group + LAG, both, 0)
+    lax.fori_loop(0, n_group + AHEAD + 1, both, 0)
 
 
 def give_back(ys, dxs, pos, ordx, ordy, p0, r1, r2, r3, n_tok):
@@ -631,7 +659,7 @@
         xs, dys, hdd, pos, bounds, order_back, p0, p1, p2, p3 = dispatch(
             x_act[0], dy_out[0], order, meta, ws_in1[0], ws_in3[0], ws_out[0], n_local, n_rows)
         recv = [lax.ppermute(part, 'expert', [(k, k ^ (2 * hop)) for k in range(n_group)]) for hop, part in ((1, p1), (2, p2), (3, p3))]
-        ys, dxs, g1, g3, g2 = experts(bounds[0, :, 0], bounds[1, :, 0], xs, dys, hdd,
+        ys, dxs, g1, g3, g2 = experts(bounds, xs, dys, hdd,
                                       w_in1[0], w_in3[0], w_out[0], ws_in1[0], ws_in3[0], ws_out[0])
         y_tok, dx_tok, f1, f3, f2 = give_back(ys, dxs, pos, order, order_back, p0, *recv, n_tok)
         return (y_tok[None], dx_tok[None], g1[None], g3[None], g2[None], f1[None], f3[None], f2[None])

time: 335 us -> 325 us (0.970)
  Pallas kernels: 312 us -> 303 us
    pallas_call x1, Pallas kernels: 129 us -> 120 us  [dispatch(): pl.pallas_call(functools.partial(dispatch_kernel, n_local, n_rows), out_s...]
  transfers between devices with their start and end apart: 3 -> 3, of which waited for: 0 -> 0; matrix products, arithmetic and copies ran while one was open for 0% -> 0% of each run, Pallas kernels for 18% -> 19%
where the time goes in v3:
time: 325 us; the launch traced here: 324 us
  Pallas kernels  303 us (93%)
  local copies, waits for them, and re-layouts  10.5 us (3%)
  other arithmetic  6.57 us (2%)
  starting transfers between devices  3.52 us (1%)
    pallas_call x1, Pallas kernels, give_back(): pl.pallas_call(return_kernel, out_shape=(jax.ShapeDtypeStruct((n_tok, wid...  122 us
    pallas_call x1, Pallas kernels, dispatch(): pl.pallas_call(functools.partial(dispatch_kernel, n_local, n_rows), out_s...  120 us
    pallas_call x1, Pallas kernels, experts(): pl.pallas_call(expert_kernel, in_specs=[smem_spec, any_spec, any_spec, an...  61 us
    unnamed x15, local copies, waits for them, and re-layouts  10.4 us
  transfers between devices with their start and end apart: 3, of which 0 were waited for; matrix products, arithmetic and copies ran while one was open for 0% of the time, Pallas kernels for 19%

profile of v3, /device:TPU:0, one launch (start us, length us, event | category | flops | bytes accessed | tf_op | source)
XLA Modules:
  0.0 324.5 jit_solution(12017699919931830410)
XLA Ops:
  0.6 5.9 %sort.21 = (s32[2048]{0:T(1024)S(1)}, s32[2048]{0:T(1024)}, f32[2048]{0:T(1024)S(1)}) sort(s32[2048]{0:T(1024)} %bitcast.37, s32[2048]{0:T(1024)S(1)} %iota.3, f32[2048]{0:T(1024)} %bitcast.38), dimensions={0}, to_apply=%region_0.0 | sort | flops 22528 | bytes 49152 | tf_op jit(solution)/shard_map/sort | solution.py:655
  6.5 0.1 pad.2.clone
  6.6 0.7 maximum_maximum_fusion.meta_ref
  7.3 119.9 %dispatch.1 = (bf16[2432,1024]{1,0:T(8,128)(2,1)}, bf16[2432,1024]{1,0:T(8,128)(2,1)}, bf16[2432,1280]{1,0:T(8,128)(2,1)}, s32[8,1,256]{2,1,0:T(1,128)}, s32[2,1...) custom-call(bf16[2048,1024]{1,0:T(8,128)(2,1)} %bitcast.21, ...), custom_call_target="tpu_custom_call" | custom-call | tf_op jit(solution)/shard_map/dispatch/pallas_call | solution.py:287
  127.2 1.4 collective-permute-start
  128.6 1.4 collective-permute-start.1
  130.0 0.7 collective-permute-start.2
  130.7 61.0 %experts.1 = (bf16[2432,1024]{1,0:T(8,128)(2,1)}, bf16[2432,1024]{1,0:T(8,128)(2,1)}, bf16[16,1024,384]{2,1,0:T(8,128)(2,1)}, bf16[16,1024,384]{2,1,0:T(8,128)(2,1)}, bf16[16,384,1024]{2,1,0:T(8,128)(2,1)}) custom-call(s32[2,16,128]{2,1,0:T(8,128)} %get-tuple-element.34.bounds_ref, bf16[2432,1024]{1,0:T(8,128)(2,1)} %get-tuple-element.35.xs_hbm, ...), custom_call_target="tpu_custom_call" | custom-call | flops 40000000000 | bytes 100000000 | tf_op jit(solution)/shard_map/experts/pallas_call | solution.py:438
  191.7 0.0 collective-permute-done.r1
  191.7 0.0 copy-start.4
  191.7 0.0 collective-permute-done.1.r2
  191.7 0.0 collective-permute-done.2.r3
  191.7 0.8 copy-done.4
  192.5 122.3 %give_back.1 = (bf16[2048,1024]{1,0:T(8,128)(2,1)}, bf16[2048,1024]{1,0:T(8,128)(2,1)}, bf16[1024,384]{1,0:T(8,128)(2,1)}, bf16[1024,384]{1,0:T(8,128)(2,1)}, bf16[384,1024]{1,0:T(8,128)(2,1)}) custom-call(bf16[2432,1024]{1,0:T(8,128)(2,1)} %get-tuple-element.38.ys_hbm, bf16[2432,1024]{1,0:T(8,128)(2,1)} %get-tuple-element.39.dxs_hbm, ...), custom_call_target="tpu_custom_call" | custom-call | tf_op jit(solution)/shard_map/give_back/pallas_call | solution.py:626
  314.8 0.0 copy-start
  314.9 4.8 %copy.23 = bf16[1,2048,1024]{2,1,0:T(8,128)(2,1)} copy(bf16[1,2048,1024]{2,1,0:T(8,128)(2,1)} %bitcast.24) | data formatting | bytes 8388608
  319.7 0.0 copy-done
  319.7 0.0 copy-start.3
  319.7 0.0 copy-start.2
  319.7 0.0 copy-start.1
  319.7 2.1 copy.24
  321.8 0.0 copy-done.3
  321.8 0.9 copy.25
  322.7 0.0 copy-done.2
  322.7 0.9 copy.26
  323.6 0.0 copy-done.1
  323.6 0.9 copy.27
  (3 shorter events, 0.0 us)
Async XLA Ops:
  127.2 64.5 %collective-permute-start = (f32[128,1152]{1,0:T(8,128)}, f32[128,1152]{1,0:T(8,128)S(1)}, u32[]{:S(2)}, u32[]{:S(2)}) collective-permute-start(f32[128,1152]{1,0:T(8,128)} %get-tuple-element.43), channel_id=1, source_target_pairs={{0,2},{1,3},{2,0},{3,1},{4,6},{5,7},{6,4},{7,5},{8,10},{9,11},{10,... | collective-permute-start | bytes 1769480 | tf_op jit(solution)/shard_map/ppermute | solution.py:661
  128.6 63.1 %collective-permute-start.1 = (f32[128,1152]{1,0:T(8,128)}, f32[128,1152]{1,0:T(8,128)}, u32[]{:S(2)}, u32[]{:S(2)}) collective-permute-start(f32[128,1152]{1,0:T(8,128)} %get-tuple-element.44), channel_id=1, source_target_pairs={{0,4},{1,5},{2,6},{3,7},{4,0},{5,1},{6,2},{7,3},{8,12},{9,13},{10,... | collective-permute-start | bytes 1769480 | tf_op jit(solution)/shard_map/ppermute | solution.py:661
  130.0 61.7 %collective-permute-start.2 = (f32[128,1152]{1,0:T(8,128)}, f32[128,1152]{1,0:T(8,128)}, u32[]{:S(2)}, u32[]{:S(2)}) collective-permute-start(f32[128,1152]{1,0:T(8,128)} %get-tuple-element.45), channel_id=1, source_target_pairs={{0,6},{1,7},{2,4},{3,5},{4,2},{5,3},{6,0},{7,1},{8,14},{9,15},{10,... | collective-permute-start | bytes 1769480 | tf_op jit(solution)/shard_map/ppermute | solution.py:661
  191.7 0.8 copy-start.4
  314.8 4.8 %copy-start = (bf16[2048,1024]{1,0:T(8,128)(2,1)S(1)}, bf16[2048,1024]{1,0:T(8,128)(2,1)}, u32[]{:S(2)}) copy-start(bf16[2048,1024]{1,0:T(8,128)(2,1)} %get-tuple-element.47) | copy-start | bytes 12582916
  319.7 2.1 copy-start.3
  319.7 3.0 copy-start.2
  319.7 3.9 %copy-start.1 = (bf16[384,1024]{1,0:T(8,128)(2,1)S(1)}, bf16[384,1024]{1,0:T(8,128)(2,1)}, u32[]{:S(2)}) copy-start(bf16[384,1024]{1,0:T(8,128)(2,1)} %get-tuple-element.53) | copy-start | bytes 2359300
